TPU v7x, 8 devices: a whole 2x2x1 slice. The times are simulated.
8 devices in a mesh: rep: 1 (over z), grp: 8 (over y, x, core).
Axes of the slice: x: 2, y: 2, z: 1, core: 2. Of those that a mesh axis runs over, the one named last changes fastest.
Arguments:
- x_in: bfloat16 [512, 2048], P(('rep', 'grp'))
- seq_len: int32 [512], P(('rep', 'grp'))
- k_cache: bfloat16 [512, 512, 2, 128], P(('rep', 'grp'))
- v_cache: bfloat16 [512, 512, 2, 128], P(('rep', 'grp'))
- gamma_attn: bfloat16 [2048], replicated
- w_qkv: bfloat16 [2048, 2560], replicated
- b_qkv: bfloat16 [2560], replicated
- w_proj: bfloat16 [2048, 2048], replicated
- gamma_mlp: bfloat16 [2048], replicated
- w_in: bfloat16 [2, 11008, 2048], P(None, 'grp')
- w_out: bfloat16 [11008, 2048], P('grp')
Outputs:
- output 1: bfloat16 [512, 2048], P(('rep', 'grp'))
- output 2: bfloat16 [512, 512, 2, 128], P(('rep', 'grp'))
- output 3: bfloat16 [512, 512, 2, 128], P(('rep', 'grp'))
All inputs are finite; a program needn't handle non-finite values.
Results may differ from a plain program's by a relative error of at most 0.00822354.
Values are sent between devices in bfloat16 or wider.
A program may use at most 1 GiB of HBM per device.

v0:
```python
import jax
import jax.numpy as jnp
from jax import lax
from jax.sharding import PartitionSpec as P

HEAD_DIM = 128
ROPE_BASE = 10000.0
EPS = 1e-5


def rms_norm(vals, gain):
    mean_sq = jnp.mean(vals * vals, axis=-1, keepdims=True)
    return (vals * lax.rsqrt(mean_sq + EPS) * gain.astype(jnp.float32)).astype(jnp.bfloat16)


def rotary(vals, positions):
    rot_dim = HEAD_DIM // 2
    inv_freq = ROPE_BASE ** (-jnp.arange(0, rot_dim, 2, dtype=jnp.float32) / rot_dim)
    angles = positions.astype(jnp.float32)[:, None] * inv_freq[None, :]
    cosine = jnp.cos(angles)[:, None, :]
    sine = jnp.sin(angles)[:, None, :]
    pairs = vals[..., :rot_dim].reshape(vals.shape[:-1] + (rot_dim // 2, 2))
    even_part = pairs[..., 0]
    odd_part = pairs[..., 1]
    rotated = jnp.stack([even_part * cosine - odd_part * sine, odd_part * cosine + even_part * sine], axis=-1)
    return jnp.concatenate([rotated.reshape(vals.shape[:-1] + (rot_dim,)), vals[..., rot_dim:]], axis=-1)


def attention_block(x_in, seq_len, k_cache, v_cache, gamma_attn, w_qkv, b_qkv, w_proj):
    batch_rows, cache_len, kv_heads = k_cache.shape[0], k_cache.shape[1], k_cache.shape[2]
    num_heads = w_proj.shape[0] // HEAD_DIM
    q_width = num_heads * HEAD_DIM
    kv_width = kv_heads * HEAD_DIM
    x_f32 = x_in.astype(jnp.float32)
    normed = rms_norm(x_f32, gamma_attn)
    qkv_proj = jnp.dot(normed, w_qkv, preferred_element_type=jnp.float32) + b_qkv.astype(jnp.float32)
    query_rot = rotary(qkv_proj[:, :q_width].reshape(batch_rows, num_heads, HEAD_DIM), seq_len).astype(jnp.bfloat16)
    key_new = rotary(qkv_proj[:, q_width:q_width + kv_width].reshape(batch_rows, kv_heads, HEAD_DIM), seq_len).astype(jnp.bfloat16)
    value_new = qkv_proj[:, q_width + kv_width:].reshape(batch_rows, kv_heads, HEAD_DIM).astype(jnp.bfloat16)
    positions = jnp.arange(cache_len, dtype=jnp.int32)
    at_len = (positions[None, :] == seq_len[:, None])[:, :, None, None]
    k_out = jnp.where(at_len, key_new[:, None], k_cache)
    v_out = jnp.where(at_len, value_new[:, None], v_cache)
    q_grouped = query_rot.reshape(batch_rows, kv_heads, num_heads // kv_heads, HEAD_DIM)
    attn_scores = jnp.einsum('bgqd,blgd->bgql', q_grouped, k_out, preferred_element_type=jnp.float32) * HEAD_DIM ** -0.5
    visible = (positions[None, :] <= seq_len[:, None])[:, None, None, :]
    attn_probs = jax.nn.softmax(jnp.where(visible, attn_scores, -jnp.inf), axis=-1).astype(jnp.bfloat16)
    context = jnp.einsum('bgql,blgd->bgqd', attn_probs, v_out, preferred_element_type=jnp.float32)
    context = context.astype(jnp.bfloat16).reshape(batch_rows, q_width)
    hidden = x_f32 + jnp.dot(context, w_proj, preferred_element_type=jnp.float32)
    return hidden, k_out, v_out


def solution(mesh):
    row_spec = P(('rep', 'grp'))
    repl_spec = P()

    def local_layer(x_in, seq_len, k_cache, v_cache, gamma_attn, w_qkv, b_qkv, w_proj, gamma_mlp, w_in, w_out):
        hidden, k_out, v_out = attention_block(x_in, seq_len, k_cache, v_cache, gamma_attn, w_qkv, b_qkv, w_proj)
        mlp_in = rms_norm(hidden, gamma_mlp)
        group_rows = lax.all_gather(mlp_in, 'grp', axis=0, tiled=True)
        gate_up = jnp.einsum('bh,cfh->bcf', group_rows, w_in, preferred_element_type=jnp.float32)
        swiglu = (jax.nn.silu(gate_up[:, 0]) * gate_up[:, 1]).astype(jnp.bfloat16)
        part_sum = jnp.dot(swiglu, w_out, preferred_element_type=jnp.float32).astype(jnp.bfloat16)
        mlp_out = lax.psum_scatter(part_sum, 'grp', scatter_dimension=0, tiled=True)
        layer_out = (hidden + mlp_out.astype(jnp.float32)).astype(jnp.bfloat16)
        return layer_out, k_out, v_out

    return jax.shard_map(local_layer, mesh=mesh,
                         in_specs=(row_spec, row_spec, row_spec, row_spec, repl_spec, repl_spec, repl_spec,
                                   repl_spec, repl_spec, P(None, 'grp', None), P('grp', None)),
                         out_specs=(row_spec, row_spec, row_spec), check_vma=False)
```

profile of v0, /device:TPU:0, one launch (start us, length us, event | category | flops | bytes accessed | tf_op | source)
XLA Modules:
  0.0 175.2 jit_solution(17025708306693581975)
XLA Ops:
  7.2 0.0 all-gather.2.cloned.1.call-start
  7.2 0.7 convert_element_type.59
  7.9 0.8 iota_compare_fusion.1
  8.6 1.1 fusion.19
  9.8 0.7 convert_element_type.56
  10.5 0.7 convert_element_type.58
  11.2 6.1 %convolution_add_fusion = f32[64,2560]{1,0:T(8,128)S(1)} fusion(bf16[2048,2560]{1,0:T(8,128)(2,1)} %param.16, f32[2560]{0:T(1024)S(1)} %convert_element_type.58, bf16[64,2048]{1,0:T(8,128)(2,1)} %param.11, f32[2048]{0:T(1024)S(1)} %convert_element_type.56, f32[64]{0:T(128)S(1)} %add_rsqrt_fusion.1), kind=kOutput, calls=%fused_computation.7 | convolution fusion | flops 671776768 | bytes 11421952 | tf_op jit(solution)/shard_map/dot_general | solution.py:36
  17.4 0.1 copy.41
  17.5 0.1 slice.64
  17.6 0.1 copy.32
  17.7 0.1 multiply_cosine_fusion
  17.9 0.1 subtract_convert_fusion.1
  18.0 0.1 pad_maximum_fusion.1
  18.1 0.1 copy.34
  18.2 0.1 pad_maximum_fusion.2
  18.3 0.1 fusion.22
  18.5 0.4 copy.38
  18.8 0.1 subtract_convert_fusion
  18.9 0.1 pad_maximum_fusion
  19.0 0.4 copy.31
  19.4 46.0 %broadcast_select_fusion.1 = (bf16[64,512,2,128]{3,2,1,0:T(2,128)(2,1)}, bf16[64,512,2,128]{3,2,1,0:T(2,128)(2,1)}) fusion(bf16[64,512,2,128]{3,2,1,0:T(2,128)(2,1)} %param.13, pred[64,512]{1,0:T(8,128)(4,1)S(1)} %get-tuple-element.12, bf16[64,2,128]{2,1,0:T(2,128)(2,1)S(1)} %copy.35, bf16[64,512,2,128]{3,2,1,0:T(2,128)(2,1)} %param.14, ...), kind=kLoop, calls=%fused_computation.2 | loop fusion | flops 16777216 | bytes 67207168 | tf_op jit(solution)/shard_map/jit(_where)/select_n | solution.py:42
  65.3 11.7 %fusion.35 = (f32[64,2,8]{2,1,0:T(2,128)S(1)}, f32[64,2,8,512]{3,2,1,0:T(8,128)}) fusion(pred[64,512]{1,0:T(8,128)(4,1)S(1)} %get-tuple-element.11, bf16[64,512,2,128]{3,2,1,0:T(2,128)(2,1)} %get-tuple-element.7, bf16[64,2,8,64]{3,2,1,0:T(8,128)(2,1)S(1)} %fusion.22, bf16[64,2,8,64]{3,2,1,0:T(8,128)(2,1)S(1)} %copy.31), kind=kOutput, calls=%fused_computation.64 | convolution fusion | flops 136839680 | bytes 19173376 | tf_op jit(solution)/shard_map/sub | solution.py:47
  77.1 8.8 %fusion.12 = bf16[64,2,8,128]{3,2,1,0:T(8,128)(2,1)S(1)} fusion(bf16[64,512,2,128]{3,2,1,0:T(2,128)(2,1)} %get-tuple-element.8, f32[64,2,8,512]{3,2,1,0:T(8,128)} %get-tuple-element.14, f32[64,2,8]{2,1,0:T(2,128)S(1)} %get-tuple-element.13), kind=kOutput, calls=%fused_computation.21 | convolution fusion | flops 135397376 | bytes 19140608 | tf_op jit(solution)/shard_map/bgql,blgd->bgqd/dot_general | solution.py:48
  85.9 5.1 %multiply_reduce_fusion = (f32[64]{0:T(128)S(1)}, f32[64,2048]{1,0:T(8,128)S(1)}) fusion(bf16[2048,2048]{1,0:T(8,128)(2,1)} %param.18, bf16[8,8,16,128]{3,2,1,0:T(8,128)(2,1)S(1)} %bitcast.43, bf16[64,2048]{1,0:T(8,128)(2,1)S(1)} %copy-done), kind=kOutput, calls=%fused_computation.35 | convolution fusion | flops 537395136 | bytes 9437440 | tf_op jit(solution)/shard_map/dot_general | solution.py:50
  91.0 0.8 multiply_convert_fusion
  91.8 0.0 all-gather.2.cloned.1.call-update
  91.8 0.2 reduce-scatter.2.cloned.1.call-start
  92.0 24.7 %all-gather.2.cloned.1.call-done = bf16[512,2048]{1,0:T(8,128)(2,1)} async-done(((bf16[64,2048]{1,0:T(8,128)(2,1)}), bf16[512,2048]{1,0:T(8,128)(2,1)}) %all-gather.2.cloned.1.call-update) | async-done | bytes 2097168 | tf_op jit(solution)/shard_map/all_gather | solution.py:61
  116.7 9.6 %fusion.7 = f32[512,2,1376]{0,2,1:T(8,128)S(1)} fusion(bf16[2,1376,2048]{2,1,0:T(8,128)(2,1)} %param.20, bf16[512,2048]{1,0:T(8,128)(2,1)} %all-gather.2.cloned.1.call-done), kind=kOutput, calls=%fused_computation.14 | convolution fusion | flops 5771362304 | bytes 19005440 | tf_op jit(solution)/shard_map/bh,cfh->bcf/dot_general | solution.py:62
  126.4 7.5 %convolution_convert_fusion = bf16[512,2048]{1,0:T(8,128)(2,1)} fusion(bf16[1376,2048]{1,0:T(8,128)(2,1)} %param.21, f32[512,2,1376]{0,2,1:T(8,128)S(1)} %fusion.7), kind=kOutput, calls=%fused_computation.8 | convolution fusion | flops 2890956800 | bytes 13369344 | tf_op jit(solution)/shard_map/dot_general | solution.py:64
  134.0 32.7 %reduce-scatter.2.cloned.1.call-done = bf16[64,2048]{1,0:T(8,128)(2,1)} async-done(((bf16[512,2048]{1,0:T(8,128)(2,1)}), bf16[64,2048]{1,0:T(8,128)(2,1)}) %reduce-scatter.2.cloned.1.call-update) | async-done | bytes 262160 | tf_op jit(solution)/shard_map/reduce_scatter | solution.py:65
  166.7 1.7 add_convert_fusion
  (16 shorter events, 0.2 us)
Async XLA Ops:
  7.2 109.6 %all-gather.2.cloned.1.call-start = ((), (), s32[]{:S(2)}) async-start(), calls=%async_computation.1 | async-start | bytes 2359296 | tf_op jit(solution)/shard_map/all_gather | solution.py:61
  11.2 6.2 %copy-start.1 = (bf16[2048]{0:T(1024)(128)(2,1)S(1)}, bf16[2048]{0:T(1024)(128)(2,1)}, u32[]{:S(2)}) copy-start(bf16[2048]{0:T(1024)(128)(2,1)} %param.19) | copy-start | bytes 12292
  77.1 8.8 %copy-start = (bf16[64,2048]{1,0:T(8,128)(2,1)S(1)}, bf16[64,2048]{1,0:T(8,128)(2,1)}, u32[]{:S(2)}) copy-start(bf16[64,2048]{1,0:T(8,128)(2,1)} %param.11) | copy-start | bytes 786436
  91.8 74.9 %reduce-scatter.2.cloned.1.call-start = ((), (), s32[]{:S(2)}) async-start(), calls=%async_computation.2 | async-start | bytes 2359296 | tf_op jit(solution)/shard_map/reduce_scatter | solution.py:65
Sparse Core Ops, SparseCore 0:
  91.9 24.7 all-gather.1
  134.1 32.5 reduce-scatter.1
where the time goes:
time: 176 us; the launch traced here: 175 us
  waiting for transfers between devices  57.5 us (33%)
  other arithmetic  53 us (30%)
  matrix products  48.8 us (28%)
  between operations  14.3 us (8%)
    select_n x1, other arithmetic, attention_block(): k_out = jnp.where(at_len, key_new[:, None], k_cache)  46 us
    reduce_scatter x1, waiting for transfers between devices, local_layer(): mlp_out = lax.psum_scatter(part_sum, 'grp', scatter_dimension=0, tiled=True)  32.7 us
    all_gather x1, waiting for transfers between devices, local_layer(): group_rows = lax.all_gather(mlp_in, 'grp', axis=0, tiled=True)  24.7 us
    sub x1, matrix products, attention_block(): jax.nn.softmax(jnp.where(visible, attn_scores, -jnp.inf), axis=-1)  11.7 us
    dot_general x1, matrix products, local_layer(): jnp.einsum('bh,cfh->bcf', group_rows, w_in, preferred_element_type=jnp.fl...  9.65 us
    dot_general x1, matrix products, attention_block(): jnp.einsum('bgql,blgd->bgqd', attn_probs, v_out, preferred_element_type=j...  8.77 us
    dot_general x1, matrix products, local_layer(): jnp.dot(swiglu, w_out, preferred_element_type=jnp.float32)  7.53 us
    dot_general x1, matrix products, attention_block(): jnp.dot(normed, w_qkv, preferred_element_type=jnp.float32)  6.08 us
  transfers between devices with their start and end apart: 2, of which 2 were waited for; matrix products, arithmetic and copies ran while one was open for 0% of the time, Pallas kernels for 0%

commit v1 on v0

v1 whole, which is shorter than its diff:
```python
import functools
import jax
import jax.numpy as jnp
import numpy as np
from jax import lax
from jax.experimental import pallas as pl
from jax.experimental.pallas import tpu as pltpu
from jax.sharding import PartitionSpec as P

HEAD = 128
ROT = 64
EPS = 1e-5
SCALE = HEAD ** -0.5


def attn_kernel(len_ref, freq_ref, x_ref, ga_ref, wq_hbm, bq_ref, wp_hbm, gm_ref, kc_hbm, vc_hbm,
                hid_ref, m_ref, ko_hbm, vo_hbm,
                kbuf, vbuf, wq, wp, n_s, lens_s, q_s, kn_s, vn_s, ctx_s, ctxb_s,
                wq_sem, wp_sem, kin_sem, vin_sem, kout_sem, vout_sem,
                *, rows, blk, heads, groups, qc):
    nblk = rows // blk
    hid = x_ref.shape[1]
    keys = kbuf.shape[1]
    nq = wq.shape[1] // qc

    def wq_copy(c):
        return pltpu.make_async_copy(wq_hbm.at[:, pl.ds(c * qc, qc)], wq.at[:, pl.ds(c * qc, qc)], wq_sem.at[c])

    def kv_in(i):
        sl = pl.ds(i * blk, blk)
        return (pltpu.make_async_copy(kc_hbm.at[sl], kbuf.at[sl], kin_sem.at[i]),
                pltpu.make_async_copy(vc_hbm.at[sl], vbuf.at[sl], vin_sem.at[i]))

    def kv_out(i):
        sl = pl.ds(i * blk, blk)
        return (pltpu.make_async_copy(kbuf.at[sl], ko_hbm.at[sl], kout_sem.at[i]),
                pltpu.make_async_copy(vbuf.at[sl], vo_hbm.at[sl], vout_sem.at[i]))

    wp_copy = pltpu.make_async_copy(wp_hbm, wp, wp_sem)

    for c in range(nq):
        wq_copy(c).start()
    for i in range(min(2, nblk)):
        for cp in kv_in(i):
            cp.start()

    for b in range(rows):
        lens_s[pl.ds(b, 1), :] = jnp.full((1, HEAD), len_ref[b].astype(jnp.float32), jnp.float32)
    x32 = x_ref[...].astype(jnp.float32)
    ms = jnp.mean(x32 * x32, axis=-1, keepdims=True)
    n_s[...] = (x32 * lax.rsqrt(ms + EPS) * ga_ref[...].astype(jnp.float32)).astype(jnp.bfloat16)
    ang = lens_s[...] * freq_ref[...]
    cos = jnp.cos(ang)
    sin = jnp.sin(ang)
    lane = lax.broadcasted_iota(jnp.int32, (rows, HEAD), 1)
    even = (lane % 2) == 0
    sin = jnp.where(even, -sin, sin)

    def rot(v):
        swapped = jnp.where(even, pltpu.roll(v, HEAD - 1, 1), pltpu.roll(v, 1, 1))
        return v * cos + swapped * sin

    nxt = min(2, nblk)
    for c in range(nq):
        wq_copy(c).wait()
        if nxt < nblk and c % 2 == 1:
            for cp in kv_in(nxt):
                cp.start()
            nxt += 1
        out = jnp.dot(n_s[...], wq[:, c * qc:(c + 1) * qc], preferred_element_type=jnp.float32)
        out = out + bq_ref[:, c * qc:(c + 1) * qc].astype(jnp.float32)
        for t in range(qc // HEAD):
            hh = c * (qc // HEAD) + t
            part = out[:, t * HEAD:(t + 1) * HEAD]
            if hh < heads:
                q_s[pl.ds(hh, rows, stride=heads), :] = rot(part)
            elif hh < heads + groups:
                kn_s[pl.ds(hh - heads, rows, stride=groups), :] = rot(part)
            else:
                vn_s[pl.ds(hh - heads - groups, rows, stride=groups), :] = part
    while nxt < nblk:
        for cp in kv_in(nxt):
            cp.start()
        nxt += 1
    wp_copy.start()

    col = lax.broadcasted_iota(jnp.int32, (heads, keys), 1)
    row = lax.broadcasted_iota(jnp.int32, (heads, keys), 0)
    own = (col % groups) == (row // (heads // groups))
    pos = jnp.where(own, col // groups, keys)
    r16 = lax.broadcasted_iota(jnp.int32, (16, HEAD), 0)
    r_pos = r16 // groups
    r_first = (r16 % groups) == 0

    def insert(buf, new_s, b, length):
        base = pl.multiple_of((length // 8) * 16, 16)
        old = buf[b, pl.ds(base, 16), :]
        new = jnp.where(r_first, new_s[pl.ds(2 * b, 1), :], new_s[pl.ds(2 * b + 1, 1), :])
        buf[b, pl.ds(base, 16), :] = jnp.where(r_pos == length % 8, new, old.astype(jnp.float32)).astype(jnp.bfloat16)

    def block(i, carry):
        for cp in kv_in(i):
            cp.wait()
        for j in range(blk):
            b = i * blk + j
            length = len_ref[b]
            insert(kbuf, kn_s, b, length)
            insert(vbuf, vn_s, b, length)
        for j in range(blk):
            b = i * blk + j
            length = len_ref[b]
            q = q_s[pl.ds(b * heads, heads), :].astype(jnp.bfloat16)
            s = lax.dot_general(q, kbuf[b], (((1,), (1,)), ((), ())), preferred_element_type=jnp.float32)
            s = jnp.where(pos <= length, s * SCALE, -jnp.inf)
            p = jnp.exp(s - jnp.max(s, axis=-1, keepdims=True))
            p = p / jnp.sum(p, axis=-1, keepdims=True)
            ctx_s[pl.ds(b * heads, heads), :] = jnp.dot(p.astype(jnp.bfloat16), vbuf[b],
                                                        preferred_element_type=jnp.float32)
        for cp in kv_out(i):
            cp.start()
        return carry

    lax.fori_loop(0, nblk, block, 0)

    for h in range(heads):
        ctxb_s[:, h * HEAD:(h + 1) * HEAD] = ctx_s[pl.ds(h, rows, stride=heads), :].astype(jnp.bfloat16)
    wp_copy.wait()
    pc = 512
    for c in range(hid // pc):
        sl = slice(c * pc, (c + 1) * pc)
        hid_ref[:, sl] = x_ref[:, sl].astype(jnp.float32) + jnp.dot(
            ctxb_s[...], wp[:, sl], preferred_element_type=jnp.float32)
    h32 = hid_ref[...]
    ms = jnp.mean(h32 * h32, axis=-1, keepdims=True)
    m_ref[...] = (h32 * lax.rsqrt(ms + EPS) * gm_ref[...].astype(jnp.float32)).astype(jnp.bfloat16)

    def drain(i, carry):
        for cp in kv_out(i):
            cp.wait()
        return carry

    lax.fori_loop(0, nblk, drain, 0)


def attention(x, lens, kc, vc, ga, wqkv, bqkv, wproj, gm):
    rows, hid = x.shape
    cache_len, groups = kc.shape[1], kc.shape[2]
    heads = wproj.shape[0] // HEAD
    blk, qc = 8, 256
    nblk = rows // blk
    freq = np.zeros((1, HEAD), np.float32)
    freq[0, :ROT] = np.repeat(np.float32(10000.0) ** (-np.arange(0, ROT, 2, dtype=np.float32) / np.float32(ROT)), 2)
    keys = cache_len * groups
    kflat = kc.reshape(rows, keys, HEAD)
    vflat = vc.reshape(rows, keys, HEAD)
    vm = pl.BlockSpec(memory_space=pltpu.VMEM)
    hbm = pl.BlockSpec(memory_space=pl.ANY)
    sm = pl.BlockSpec(memory_space=pltpu.SMEM)
    bf, f32 = jnp.bfloat16, jnp.float32
    hidden, m, ko, vo = pl.pallas_call(
        functools.partial(attn_kernel, rows=rows, blk=blk, heads=heads, groups=groups, qc=qc),
        name="attn",
        out_shape=(jax.ShapeDtypeStruct((rows, hid), f32), jax.ShapeDtypeStruct((rows, hid), bf),
                   jax.ShapeDtypeStruct(kflat.shape, bf), jax.ShapeDtypeStruct(vflat.shape, bf)),
        in_specs=[sm, vm, vm, vm, hbm, vm, hbm, vm, hbm, hbm],
        out_specs=(vm, vm, hbm, hbm),
        scratch_shapes=[
            pltpu.VMEM((rows, keys, HEAD), bf), pltpu.VMEM((rows, keys, HEAD), bf),
            pltpu.VMEM(wqkv.shape, bf), pltpu.VMEM(wproj.shape, bf),
            pltpu.VMEM((rows, hid), bf), pltpu.VMEM((rows, HEAD), f32),
            pltpu.VMEM((rows * heads, HEAD), f32),
            pltpu.VMEM((rows * groups, HEAD), f32), pltpu.VMEM((rows * groups, HEAD), f32),
            pltpu.VMEM((rows * heads, HEAD), f32), pltpu.VMEM((rows, heads * HEAD), bf),
            pltpu.SemaphoreType.DMA((wqkv.shape[1] // qc,)), pltpu.SemaphoreType.DMA(()),
            pltpu.SemaphoreType.DMA((nblk,)), pltpu.SemaphoreType.DMA((nblk,)),
            pltpu.SemaphoreType.DMA((nblk,)), pltpu.SemaphoreType.DMA((nblk,)),
        ],
        compiler_params=pltpu.CompilerParams(vmem_limit_bytes=60 * 1024 * 1024),
        cost_estimate=pl.CostEstimate(flops=2 * rows * hid * 4608 + 4 * rows * heads * keys * HEAD,
                                      bytes_accessed=86000000, transcendentals=rows * heads * keys),
    )(lens, jnp.asarray(freq), x, ga.reshape(1, -1), wqkv, bqkv.reshape(1, -1), wproj, gm.reshape(1, -1), kflat, vflat)
    return hidden, m, ko.reshape(kc.shape), vo.reshape(vc.shape)


def solution(mesh):
    row_spec = P(('rep', 'grp'))
    repl_spec = P()

    def local_layer(x_in, seq_len, k_cache, v_cache, gamma_attn, w_qkv, b_qkv, w_proj, gamma_mlp, w_in, w_out):
        hidden, mlp_in, k_out, v_out = attention(x_in, seq_len, k_cache, v_cache, gamma_attn, w_qkv, b_qkv, w_proj, gamma_mlp)
        group_rows = lax.all_gather(mlp_in, 'grp', axis=0, tiled=True)
        gate_up = jnp.einsum('bh,cfh->bcf', group_rows, w_in, preferred_element_type=jnp.float32)
        swiglu = (jax.nn.silu(gate_up[:, 0]) * gate_up[:, 1]).astype(jnp.bfloat16)
        part_sum = jnp.dot(swiglu, w_out, preferred_element_type=jnp.float32).astype(jnp.bfloat16)
        mlp_out = lax.psum_scatter(part_sum, 'grp', scatter_dimension=0, tiled=True)
        layer_out = (hidden + mlp_out.astype(jnp.float32)).astype(jnp.bfloat16)
        return layer_out, k_out, v_out

    return jax.shard_map(local_layer, mesh=mesh,
                         in_specs=(row_spec, row_spec, row_spec, row_spec, repl_spec, repl_spec, repl_spec,
                                   repl_spec, repl_spec, P(None, 'grp', None), P('grp', None)),
                         out_specs=(row_spec, row_spec, row_spec), check_vma=False)
```

time: 176 us -> 132 us (0.75)
  other arithmetic: 53 us -> 1.7 us
  Pallas kernels: 0 us -> 36.3 us
  matrix products: 48.8 us -> 17.2 us
  local copies, waits for them, and re-layouts: 1.42 us -> 3.88 us
    select_n x1 -> x0, other arithmetic: 46 us -> none  [attention_block(): k_out = jnp.where(at_len, key_new[:, None], k_cache)]
    pallas_call x0 -> x1, Pallas kernels: none -> 36.3 us  [attention(): pl.pallas_call(functools.partial(attn_kernel, rows=rows, blk=blk, heads=h...]
    dot_general x3 -> x0, matrix products: 19.9 us -> none  [the longest x1 8.77 us: attention_block(): jnp.einsum('bgql,blgd->bgqd', attn_probs, v_out, preferred_element_type=j...]
    sub x1 -> x0, matrix products: 11.7 us -> none  [attention_block(): jax.nn.softmax(jnp.where(visible, attn_scores, -jnp.inf), axis=-1)]
    reshape x1 -> x3, local copies, waits for them, and re-layouts: 0.04 us -> 3.87 us  [the longest x1 1.3 us: attention(): ga.reshape(1, -1)]
    convert_element_type x5 -> x0, other arithmetic: 2.89 us -> none  [the longest x1 0.83 us: rms_norm(): (vals * lax.rsqrt(mean_sq + EPS) * gain.astype(jnp.float32)).astype(jnp.b...]
where the time goes in v1:
time: 132 us; the launch traced here: 131 us
  waiting for transfers between devices  58.1 us (44%)
  Pallas kernels  36.3 us (27%)
  matrix products  17.2 us (13%)
  between operations  14.1 us (11%)
  local copies, waits for them, and re-layouts  3.88 us (3%)
  other arithmetic  1.7 us (1%)
    pallas_call x1, Pallas kernels, attention(): pl.pallas_call(functools.partial(attn_kernel, rows=rows, blk=blk, heads=h...  36.3 us
    reduce_scatter x1, waiting for transfers between devices, local_layer(): mlp_out = lax.psum_scatter(part_sum, 'grp', scatter_dimension=0, tiled=True)  32.9 us
    all_gather x1, waiting for transfers between devices, local_layer(): group_rows = lax.all_gather(mlp_in, 'grp', axis=0, tiled=True)  25.1 us
    dot_general x1, matrix products, local_layer(): jnp.einsum('bh,cfh->bcf', group_rows, w_in, preferred_element_type=jnp.fl...  9.64 us
    dot_general x1, matrix products, local_layer(): jnp.dot(swiglu, w_out, preferred_element_type=jnp.float32)  7.57 us
  transfers between devices with their start and end apart: 2, of which 2 were waited for; matrix products, arithmetic and copies ran while one was open for 0% of the time, Pallas kernels for 0%

profile of v1, /device:TPU:0, one launch (start us, length us, event | category | flops | bytes accessed | tf_op | source)
XLA Modules:
  0.0 131.3 jit_solution(18047621144082685620)
XLA Ops:
  7.2 0.0 all-gather.2.cloned.1.call-start
  7.2 1.3 reshape.27.ga_ref
  8.5 1.3 reshape.29.gm_ref
  9.8 1.3 reshape.28.bq_ref
  11.1 36.3 %attn.1 = (f32[64,2048]{1,0:T(8,128)}, bf16[64,2048]{1,0:T(8,128)(2,1)}, bf16[64,1024,128]{2,1,0:T(8,128)(2,1)}, bf16[64,1024,128]{2,1,0:T(8,128)(2,1)}) custom-call(s32[64]{0:T(128)} %len_ref.1, f32[1,128]{1,0:T(1,128)} %constant.5.clone.freq_ref, bf16[64,2048]{1,0:T(8,128)(2,1)} %x_ref.1, bf16[1,2048]{1,0:T(2,128)(2,1)} %reshape.27.ga_ref, ...), custom_call_target="tpu_custom_call" | custom-call | flops 1744830464 | bytes 86000000 | tf_op jit(solution)/shard_map/attn/pallas_call | solution.py:160
  47.4 0.0 all-gather.2.cloned.1.call-update
  47.4 0.0 reduce-scatter.2.cloned.1.call-start
  47.5 25.1 %all-gather.2.cloned.1.call-done = bf16[512,2048]{1,0:T(8,128)(2,1)} async-done(((bf16[64,2048]{1,0:T(8,128)(2,1)}), bf16[512,2048]{1,0:T(8,128)(2,1)}) %all-gather.2.cloned.1.call-update) | async-done | bytes 2097168 | tf_op jit(solution)/shard_map/all_gather | solution.py:191
  72.6 9.6 %fusion.2 = f32[512,2,1376]{0,2,1:T(8,128)S(1)} fusion(bf16[2,1376,2048]{2,1,0:T(8,128)(2,1)} %param.21, bf16[512,2048]{1,0:T(8,128)(2,1)} %all-gather.2.cloned.1.call-done), kind=kOutput, calls=%fused_computation.5 | convolution fusion | flops 5771362304 | bytes 19005440 | tf_op jit(solution)/shard_map/bh,cfh->bcf/dot_general | solution.py:192
  82.2 0.0 copy-start
  82.2 7.6 %convolution_convert_fusion = bf16[512,2048]{1,0:T(8,128)(2,1)} fusion(bf16[1376,2048]{1,0:T(8,128)(2,1)} %param.22, f32[512,2,1376]{0,2,1:T(8,128)S(1)} %fusion.2), kind=kOutput, calls=%fused_computation | convolution fusion | flops 2890956800 | bytes 13369344 | tf_op jit(solution)/shard_map/dot_general | solution.py:194
  89.8 0.0 reduce-scatter.2.cloned.1.call-update
  89.8 32.9 %reduce-scatter.2.cloned.1.call-done = bf16[64,2048]{1,0:T(8,128)(2,1)} async-done(((bf16[512,2048]{1,0:T(8,128)(2,1)}), bf16[64,2048]{1,0:T(8,128)(2,1)}) %reduce-scatter.2.cloned.1.call-update) | async-done | bytes 262160 | tf_op jit(solution)/shard_map/reduce_scatter | solution.py:195
  122.8 0.0 copy-done
  122.8 1.7 %add_convert_fusion = bf16[64,2048]{1,0:T(8,128)(2,1)} fusion(f32[64,2048]{1,0:T(8,128)S(1)} %copy-done, bf16[64,2048]{1,0:T(8,128)(2,1)} %reduce-scatter.2.cloned.1.call-done), kind=kLoop, calls=%fused_computation.8 | loop fusion | flops 393216 | bytes 1048576 | tf_op jit(solution)/shard_map/convert_element_type | solution.py:196
Async XLA Ops:
  7.2 65.4 %all-gather.2.cloned.1.call-start = ((), (), s32[]{:S(2)}) async-start(), calls=%async_computation.1 | async-start | bytes 2359296 | tf_op jit(solution)/shard_map/all_gather | solution.py:191
  47.4 75.4 %reduce-scatter.2.cloned.1.call-start = ((), (), s32[]{:S(2)}) async-start(), calls=%async_computation.2 | async-start | bytes 2359296 | tf_op jit(solution)/shard_map/reduce_scatter | solution.py:195
  82.2 40.5 %copy-start = (f32[64,2048]{1,0:T(8,128)S(1)}, f32[64,2048]{1,0:T(8,128)}, u32[]{:S(2)}) copy-start(f32[64,2048]{1,0:T(8,128)} %get-tuple-element.7) | copy-start | bytes 1572868
Sparse Core Ops, SparseCore 0:
  47.5 25.0 all-gather.1
  90.0 32.7 reduce-scatter.1

commit v2 on v1

--- a/solution.py
+++ b/solution.py
@@ -182,18 +182,187 @@
     return hidden, m, ko.reshape(kc.shape), vo.reshape(vc.shape)
 
 
+def mlp_kernel(hid_ref, m_ref, wi_hbm, wo_hbm, out_ref,
+               wi, wt, wo, gath, act, own_s, ps, rb, sb, rr,
+               wi_sem, wt_sem, wo_sem, ag_send, ag_recv, fw_send, ps_send, ps_recv, rs_send, rs_recv,
+               *, chunks, crows, full, tail, fc, nc):
+    hid = m_ref.shape[1]
+    ncol = hid // nc
+    me = lax.axis_index('grp')
+    core, xx, yy = me % 2, (me // 2) % 2, me // 4
+    peer = me + 1 - 2 * core
+    near_x = me + 2 - 4 * xx
+    near_y = me + 4 - 8 * yy
+    diag = me + 2 - 4 * xx + 4 - 8 * yy
+    remote = (near_x, near_y, diag)
+
+    def wi_copy(f, g):
+        sl = pl.ds(f * fc, fc)
+        return pltpu.make_async_copy(wi_hbm.at[g, sl], wi.at[g, sl], wi_sem.at[f, g])
+
+    def wt_copy(g):
+        return pltpu.make_async_copy(wi_hbm.at[g, pl.ds(full * fc, tail)], wt.at[pl.ds(g * (fc // 2), tail)], wt_sem.at[g])
+
+    def wo_copy(c):
+        return pltpu.make_async_copy(wo_hbm.at[:, pl.ds(c * nc, nc)],
+                                     wo.at[pl.ds(0, full * fc + tail), pl.ds(c * nc, nc)], wo_sem.at[c])
+
+    for f in range(full):
+        for g in range(2):
+            wi_copy(f, g).start()
+    for g in range(2):
+        wt_copy(g).start()
+    for c in range(ncol):
+        wo_copy(c).start()
+
+    def rcopy(src, dst, ss, rs, dev):
+        return pltpu.make_async_remote_copy(src_ref=src, dst_ref=dst, send_sem=ss, recv_sem=rs,
+                                            device_id={'grp': dev}, device_id_type=pl.DeviceIdType.MESH)
+
+    def own_send(h, q):
+        slot, dev = ((4, peer), (1, near_x), (2, near_y), (3, diag))[q]
+        return rcopy(m_ref.at[pl.ds(h * crows, crows)], gath.at[h, pl.ds(slot * crows, crows)],
+                     ag_send.at[h, q], ag_recv.at[h, slot], dev)
+
+    def forward(h, q):
+        return rcopy(gath.at[h, pl.ds(q * crows, crows)], gath.at[h, pl.ds((q + 4) * crows, crows)],
+                     fw_send.at[h, q], ag_recv.at[h, q + 4], peer)
+
+    def pair_send(h, c):
+        sl = (h, slice(None), pl.ds(c * nc, nc))
+        return rcopy(ps.at[sl], rb.at[sl], ps_send.at[h, c], ps_recv.at[h, c], peer)
+
+    def part_send(h, c, q):
+        sl = (h, q, slice(None), pl.ds(c * nc, nc))
+        return rcopy(sb.at[sl], rr.at[sl], rs_send.at[h, c, q], rs_recv.at[h, c, q], remote[q])
+
+    barrier = pltpu.get_barrier_semaphore()
+    for dev in (peer,) + remote:
+        pl.semaphore_signal(barrier, inc=1, device_id={'grp': dev}, device_id_type=pl.DeviceIdType.MESH)
+    pl.semaphore_wait(barrier, 4)
+
+    for h in range(chunks):
+        for q in (1, 2, 3, 0):
+            own_send(h, q).start()
+
+    pad = fc // 2 - tail
+    for g in range(2):
+        wt[g * (fc // 2) + tail:(g + 1) * (fc // 2), :] = jnp.zeros((pad, hid), jnp.bfloat16)
+    wo[full * fc + tail:, :] = jnp.zeros((pad, hid), jnp.bfloat16)
+    for h in range(chunks):
+        gath[h, 0:crows] = m_ref[h * crows:(h + 1) * crows, :]
+
+    nt = (((1,), (1,)), ((), ()))
+
+    def pair_sum(h, c):
+        pair_send(h, c).wait_recv()
+        cs = slice(c * nc, (c + 1) * nc)
+        tot = own_s[h, :, cs] + rb[h, :, cs].astype(jnp.float32)
+        own_s[h, 0:crows, cs] = tot[0:crows]
+        for q in range(3):
+            sb[h, q, :, cs] = tot[(q + 1) * crows:(q + 2) * crows].astype(jnp.bfloat16)
+        for q in (2, 0, 1):
+            part_send(h, c, q).start()
+
+    for h in range(chunks):
+        for q in (1, 2, 3):
+            own_send(h, q).wait_recv()
+            forward(h, q).start()
+        own_send(h, 0).wait_recv()
+        for q in (1, 2, 3):
+            forward(h, q).wait_recv()
+
+        def in_proj(f, carry):
+            if h == 0:
+                for g in range(2):
+                    wi_copy(f, g).wait()
+            sl = pl.ds(pl.multiple_of(f * fc, fc), fc)
+            gate = lax.dot_general(gath[h], wi[0, sl, :], nt, preferred_element_type=jnp.float32)
+            up = lax.dot_general(gath[h], wi[1, sl, :], nt, preferred_element_type=jnp.float32)
+            act[:, sl] = (jax.nn.silu(gate) * up).astype(jnp.bfloat16)
+            return carry
+
+        lax.fori_loop(0, full, in_proj, 0)
+        if h == 0:
+            for g in range(2):
+                wt_copy(g).wait()
+        gu = lax.dot_general(gath[h], wt[...], nt, preferred_element_type=jnp.float32)
+        act[:, full * fc:] = (jax.nn.silu(gu[:, :fc // 2]) * gu[:, fc // 2:]).astype(jnp.bfloat16)
+
+        half = 4 * crows
+        for c in range(ncol):
+            if h == 0:
+                wo_copy(c).wait()
+            cs = slice(c * nc, (c + 1) * nc)
+            part = jnp.dot(act[...], wo[:, cs], preferred_element_type=jnp.float32)
+            ps[h, :, cs] = part[half:].astype(jnp.bfloat16)
+            own_s[h, :, cs] = part[:half]
+            pair_send(h, c).start()
+            if c > 0:
+                pair_sum(h, c - 1)
+        pair_sum(h, ncol - 1)
+
+    for h in range(chunks):
+        rs = slice(h * crows, (h + 1) * crows)
+        for c in range(ncol):
+            cs = slice(c * nc, (c + 1) * nc)
+            for q in range(3):
+                part_send(h, c, q).wait_recv()
+            tot = hid_ref[rs, cs] + own_s[h, 0:crows, cs]
+            for q in range(3):
+                tot = tot + rr[h, q, :, cs].astype(jnp.float32)
+            out_ref[rs, cs] = tot.astype(jnp.bfloat16)
+
+    for h in range(chunks):
+        for q in range(4):
+            own_send(h, q).wait_send()
+        for q in (1, 2, 3):
+            forward(h, q).wait_send()
+        for c in range(ncol):
+            pair_send(h, c).wait_send()
+            for q in range(3):
+                part_send(h, c, q).wait_send()
+
+
+def mlp(hidden, m, w_in, w_out):
+    rows, hid = m.shape
+    ffn = w_out.shape[0]
+    chunks, fc, nc = 2, 256, 512
+    crows = rows // chunks
+    full, tail = ffn // fc, ffn % fc
+    ncol = hid // nc
+    vm = pl.BlockSpec(memory_space=pltpu.VMEM)
+    hbm = pl.BlockSpec(memory_space=pl.ANY)
+    bf, f32 = jnp.bfloat16, jnp.float32
+    dma = pltpu.SemaphoreType.DMA
+    return pl.pallas_call(
+        functools.partial(mlp_kernel, chunks=chunks, crows=crows, full=full, tail=tail, fc=fc, nc=nc),
+        name="mlp",
+        out_shape=jax.ShapeDtypeStruct((rows, hid), bf),
+        in_specs=[vm, vm, hbm, hbm],
+        out_specs=vm,
+        scratch_shapes=[
+            pltpu.VMEM((2, full * fc, hid), bf), pltpu.VMEM((fc, hid), bf), pltpu.VMEM((full * fc + fc // 2, hid), bf),
+            pltpu.VMEM((chunks, 8 * crows, hid), bf), pltpu.VMEM((8 * crows, full * fc + fc // 2), bf),
+            pltpu.VMEM((chunks, 4 * crows, hid), f32), pltpu.VMEM((chunks, 4 * crows, hid), bf),
+            pltpu.VMEM((chunks, 4 * crows, hid), bf),
+            pltpu.VMEM((chunks, 3, crows, hid), bf), pltpu.VMEM((chunks, 3, crows, hid), bf),
+            dma((full, 2)), dma((2,)), dma((ncol,)),
+            dma((chunks, 4)), dma((chunks, 8)), dma((chunks, 4)),
+            dma((chunks, ncol)), dma((chunks, ncol)), dma((chunks, ncol, 3)), dma((chunks, ncol, 3)),
+        ],
+        compiler_params=pltpu.CompilerParams(collective_id=0, has_side_effects=True, vmem_limit_bytes=60 * 1024 * 1024),
+        cost_estimate=pl.CostEstimate(flops=2 * 8 * rows * hid * ffn * 3, bytes_accessed=17000000, transcendentals=8 * rows * ffn),
+    )(hidden, m, w_in, w_out)
+
+
 def solution(mesh):
     row_spec = P(('rep', 'grp'))
     repl_spec = P()
 
     def local_layer(x_in, seq_len, k_cache, v_cache, gamma_attn, w_qkv, b_qkv, w_proj, gamma_mlp, w_in, w_out):
         hidden, mlp_in, k_out, v_out = attention(x_in, seq_len, k_cache, v_cache, gamma_attn, w_qkv, b_qkv, w_proj, gamma_mlp)
-        group_rows = lax.all_gather(mlp_in, 'grp', axis=0, tiled=True)
-        gate_up = jnp.einsum('bh,cfh->bcf', group_rows, w_in, preferred_element_type=jnp.float32)
-        swiglu = (jax.nn.silu(gate_up[:, 0]) * gate_up[:, 1]).astype(jnp.bfloat16)
-        part_sum = jnp.dot(swiglu, w_out, preferred_element_type=jnp.float32).astype(jnp.bfloat16)
-        mlp_out = lax.psum_scatter(part_sum, 'grp', scatter_dimension=0, tiled=True)
-        layer_out = (hidden + mlp_out.astype(jnp.float32)).astype(jnp.bfloat16)
+        layer_out = mlp(hidden, mlp_in, w_in, w_out)
         return layer_out, k_out, v_out
 
     return jax.shard_map(local_layer, mesh=mesh,

time: 132 us -> 83.3 us (0.63)
  waiting for transfers between devices: 58.1 us -> 0 us
  Pallas kernels: 36.3 us -> 76.9 us
  matrix products: 17.2 us -> 0 us
  between operations: 14.1 us -> 0.65 us
  other arithmetic: 1.7 us -> 0 us
  local copies, waits for them, and re-layouts: 3.88 us -> 5.53 us
    pallas_call x0 -> x1, Pallas kernels: none -> 40.6 us  [mlp(): pl.pallas_call(functools.partial(mlp_kernel, chunks=chunks, crows=crows,...]
    reduce_scatter x1 -> x0, waiting for transfers between devices: 32.9 us -> none  [local_layer(): mlp_out = lax.psum_scatter(part_sum, 'grp', scatter_dimension=0, tiled=True)]
    all_gather x1 -> x0, waiting for transfers between devices: 25.1 us -> none  [local_layer(): group_rows = lax.all_gather(mlp_in, 'grp', axis=0, tiled=True)]
    dot_general x2 -> x0, matrix products: 17.2 us -> none  [the longest x1 9.64 us: local_layer(): jnp.einsum('bh,cfh->bcf', group_rows, w_in, preferred_element_type=jnp.fl...]
    convert_element_type x1 -> x0, other arithmetic: 1.7 us -> none  [local_layer(): layer_out = (hidden + mlp_out.astype(jnp.float32)).astype(jnp.bfloat16)]
    unnamed x2 -> x1, local copies, waits for them, and re-layouts: 0.01 us -> 1.67 us
  transfers between devices with their start and end apart: 2 -> 0, of which waited for: 2 -> 0; matrix products, arithmetic and copies ran while one was open for 0% -> 0% of each run, Pallas kernels for 0% -> 0%
where the time goes in v2:
time: 83.3 us; the launch traced here: 83.1 us
  Pallas kernels  76.9 us (92%)
  local copies, waits for them, and re-layouts  5.53 us (7%)
    pallas_call x1, Pallas kernels, mlp(): pl.pallas_call(functools.partial(mlp_kernel, chunks=chunks, crows=crows,...  40.6 us
    pallas_call x1, Pallas kernels, attention(): pl.pallas_call(functools.partial(attn_kernel, rows=rows, blk=blk, heads=h...  36.3 us
    unnamed x1, local copies, waits for them, and re-layouts  1.67 us

profile of v2, /device:TPU:0, one launch (start us, length us, event | category | flops | bytes accessed | tf_op | source)
XLA Modules:
  0.0 83.1 jit_solution(961557176187405150)
XLA Ops:
  0.6 1.3 %reshape.27.ga_ref = bf16[1,2048]{1,0:T(2,128)(2,1)} reshape(bf16[2048]{0:T(1024)(128)(2,1)} %param.16) | data formatting | bytes 8192 | tf_op jit(solution)/shard_map/reshape | solution.py:181
  1.9 1.3 %reshape.29.gm_ref = bf16[1,2048]{1,0:T(2,128)(2,1)} reshape(bf16[2048]{0:T(1024)(128)(2,1)} %param.20) | data formatting | bytes 8192 | tf_op jit(solution)/shard_map/reshape | solution.py:181
  3.2 1.3 %reshape.28.bq_ref = bf16[1,2560]{1,0:T(2,128)(2,1)} reshape(bf16[2560]{0:T(1024)(128)(2,1)} %param.18) | data formatting | bytes 10240 | tf_op jit(solution)/shard_map/reshape | solution.py:181
  4.5 36.3 %attn.1 = (f32[64,2048]{1,0:T(8,128)}, bf16[64,2048]{1,0:T(8,128)(2,1)}, bf16[64,1024,128]{2,1,0:T(8,128)(2,1)}, bf16[64,1024,128]{2,1,0:T(8,128)(2,1)}) custom-call(s32[64]{0:T(128)} %len_ref.1, f32[1,128]{1,0:T(1,128)} %constant.2.clone.freq_ref, bf16[64,2048]{1,0:T(8,128)(2,1)} %x_ref.1, bf16[1,2048]{1,0:T(2,128)(2,1)} %reshape.27.ga_ref, ...), custom_call_target="tpu_custom_call" | custom-call | flops 1744830464 | bytes 86000000 | tf_op jit(solution)/shard_map/attn/pallas_call | solution.py:160
  40.8 40.6 %mlp.1 = bf16[64,2048]{1,0:T(8,128)(2,1)} custom-call(f32[64,2048]{1,0:T(8,128)} %get-tuple-element.7.hid_ref, bf16[64,2048]{1,0:T(8,128)(2,1)} %get-tuple-element.8.m_ref, bf16[2,1376,2048]{2,1,0:T(8,128)(2,1)} %wi_hbm.1, bf16[1376,2048]{1,0:T(8,128)(2,1)} %wo_hbm.1), custom_call_target="tpu_custom_call" | custom-call | flops 8657043456 | bytes 17000000 | tf_op jit(solution)/shard_map/mlp/pallas_call | solution.py:338
  81.4 1.7 %copy.16 = bf16[64,2048]{1,0:T(8,128)(2,1)} copy(bf16[64,2048]{1,0:T(8,128)(2,1)} %mlp.1) | data formatting | bytes 524288

commit v3 on v2

--- a/solution.py
+++ b/solution.py
@@ -11,18 +11,25 @@
 ROT = 64
 EPS = 1e-5
 SCALE = HEAD ** -0.5
-
-
-def attn_kernel(len_ref, freq_ref, x_ref, ga_ref, wq_hbm, bq_ref, wp_hbm, gm_ref, kc_hbm, vc_hbm,
+WQ_AHEAD = 10
+KV_AHEAD = 4
+
+
+def attn_kernel(len_hbm, freq_hbm, x_hbm, ga_hbm, wq_hbm, bq_hbm, wp_hbm, gm_hbm, kc_hbm, vc_hbm,
                 hid_ref, m_ref, ko_hbm, vo_hbm,
-                kbuf, vbuf, wq, wp, n_s, lens_s, q_s, kn_s, vn_s, ctx_s, ctxb_s,
-                wq_sem, wp_sem, kin_sem, vin_sem, kout_sem, vout_sem,
+                kbuf, vbuf, wq, wp, len_ref, freq_ref, x_ref, ga_ref, bq_ref, gm_ref,
+                n_s, lens_s, q_s, kn_s, vn_s, s_s, p_s, ctx_s, ctxb_s,
+                small_sem, wq_sem, wp_sem, kin_sem, vin_sem, kout_sem, vout_sem,
                 *, rows, blk, heads, groups, qc):
     nblk = rows // blk
     hid = x_ref.shape[1]
     keys = kbuf.shape[1]
     nq = wq.shape[1] // qc
 
+    small = [pltpu.make_async_copy(src, dst, small_sem.at[i]) for i, (src, dst) in enumerate((
+        (x_hbm, x_ref), (len_hbm, len_ref), (ga_hbm, ga_ref), (freq_hbm, freq_ref),
+        (bq_hbm, bq_ref), (gm_hbm, gm_ref)))]
+
     def wq_copy(c):
         return pltpu.make_async_copy(wq_hbm.at[:, pl.ds(c * qc, qc)], wq.at[:, pl.ds(c * qc, qc)], wq_sem.at[c])
 
@@ -38,17 +45,21 @@
 
     wp_copy = pltpu.make_async_copy(wp_hbm, wp, wp_sem)
 
-    for c in range(nq):
+    for cp in small:
+        cp.start()
+    for c in range(min(WQ_AHEAD, nq)):
         wq_copy(c).start()
-    for i in range(min(2, nblk)):
+    for i in range(min(KV_AHEAD, nblk)):
         for cp in kv_in(i):
             cp.start()
+    for cp in small:
+        cp.wait()
 
     for b in range(rows):
         lens_s[pl.ds(b, 1), :] = jnp.full((1, HEAD), len_ref[b].astype(jnp.float32), jnp.float32)
     x32 = x_ref[...].astype(jnp.float32)
     ms = jnp.mean(x32 * x32, axis=-1, keepdims=True)
-    n_s[...] = (x32 * lax.rsqrt(ms + EPS) * ga_ref[...].astype(jnp.float32)).astype(jnp.bfloat16)
+    n_s[...] = (x32 * lax.rsqrt(ms + EPS) * ga_ref[...].astype(jnp.float32).reshape(1, hid)).astype(jnp.bfloat16)
     ang = lens_s[...] * freq_ref[...]
     cos = jnp.cos(ang)
     sin = jnp.sin(ang)
@@ -60,15 +71,18 @@
         swapped = jnp.where(even, pltpu.roll(v, HEAD - 1, 1), pltpu.roll(v, 1, 1))
         return v * cos + swapped * sin
 
-    nxt = min(2, nblk)
+    nxt = min(KV_AHEAD, nblk)
+    bias = bq_ref[...].astype(jnp.float32).reshape(1, nq * qc)
     for c in range(nq):
         wq_copy(c).wait()
-        if nxt < nblk and c % 2 == 1:
+        if c + WQ_AHEAD < nq:
+            wq_copy(c + WQ_AHEAD).start()
+        if nxt < nblk and c + WQ_AHEAD >= nq - 1:
             for cp in kv_in(nxt):
                 cp.start()
             nxt += 1
         out = jnp.dot(n_s[...], wq[:, c * qc:(c + 1) * qc], preferred_element_type=jnp.float32)
-        out = out + bq_ref[:, c * qc:(c + 1) * qc].astype(jnp.float32)
+        out = out + bias[:, c * qc:(c + 1) * qc]
         for t in range(qc // HEAD):
             hh = c * (qc // HEAD) + t
             part = out[:, t * HEAD:(t + 1) * HEAD]
@@ -91,12 +105,33 @@
     r16 = lax.broadcasted_iota(jnp.int32, (16, HEAD), 0)
     r_pos = r16 // groups
     r_first = (r16 % groups) == 0
+    zero = jnp.zeros((heads, HEAD), jnp.bfloat16)
 
     def insert(buf, new_s, b, length):
         base = pl.multiple_of((length // 8) * 16, 16)
         old = buf[b, pl.ds(base, 16), :]
         new = jnp.where(r_first, new_s[pl.ds(2 * b, 1), :], new_s[pl.ds(2 * b + 1, 1), :])
         buf[b, pl.ds(base, 16), :] = jnp.where(r_pos == length % 8, new, old.astype(jnp.float32)).astype(jnp.bfloat16)
+
+    def scores(b):
+        qa = q_s[pl.ds(b * heads, heads), :].astype(jnp.bfloat16)
+        qb = q_s[pl.ds((b + 1) * heads, heads), :].astype(jnp.bfloat16)
+        lhs = jnp.concatenate([jnp.concatenate([qa, zero], 1), jnp.concatenate([zero, qb], 1)], 0)
+        rhs = jnp.concatenate([kbuf[b], kbuf[b + 1]], 1)
+        return lax.dot_general(lhs, rhs, (((1,), (1,)), ((), ())), preferred_element_type=jnp.float32)
+
+    def softmax(s, length):
+        s = jnp.where(pos <= length, s * SCALE, -jnp.inf)
+        p = jnp.exp(s - jnp.max(s, axis=-1, keepdims=True))
+        return (p / jnp.sum(p, axis=-1, keepdims=True)).astype(jnp.bfloat16)
+
+    def values(p, b):
+        rhs = jnp.concatenate([vbuf[b], vbuf[b + 1]], 1)
+        r = jnp.dot(p, rhs, preferred_element_type=jnp.float32)
+        ctx_s[pl.ds(b * heads, heads), :] = r[:heads, :HEAD]
+        ctx_s[pl.ds((b + 1) * heads, heads), :] = r[heads:, HEAD:]
+
+    pairs = blk // 2
 
     def block(i, carry):
         for cp in kv_in(i):
@@ -106,16 +141,14 @@
             length = len_ref[b]
             insert(kbuf, kn_s, b, length)
             insert(vbuf, vn_s, b, length)
-        for j in range(blk):
-            b = i * blk + j
-            length = len_ref[b]
-            q = q_s[pl.ds(b * heads, heads), :].astype(jnp.bfloat16)
-            s = lax.dot_general(q, kbuf[b], (((1,), (1,)), ((), ())), preferred_element_type=jnp.float32)
-            s = jnp.where(pos <= length, s * SCALE, -jnp.inf)
-            p = jnp.exp(s - jnp.max(s, axis=-1, keepdims=True))
-            p = p / jnp.sum(p, axis=-1, keepdims=True)
-            ctx_s[pl.ds(b * heads, heads), :] = jnp.dot(p.astype(jnp.bfloat16), vbuf[b],
-                                                        preferred_element_type=jnp.float32)
+        for t in range(pairs):
+            s_s[t] = scores(i * blk + 2 * t)
+        for t in range(pairs):
+            b = i * blk + 2 * t
+            p_s[t, :heads, :] = softmax(s_s[t, :heads, :], len_ref[b])
+            p_s[t, heads:, :] = softmax(s_s[t, heads:, :], len_ref[b + 1])
+        for t in range(pairs):
+            values(p_s[t], i * blk + 2 * t)
         for cp in kv_out(i):
             cp.start()
         return carry
@@ -132,7 +165,7 @@
             ctxb_s[...], wp[:, sl], preferred_element_type=jnp.float32)
     h32 = hid_ref[...]
     ms = jnp.mean(h32 * h32, axis=-1, keepdims=True)
-    m_ref[...] = (h32 * lax.rsqrt(ms + EPS) * gm_ref[...].astype(jnp.float32)).astype(jnp.bfloat16)
+    m_ref[...] = (h32 * lax.rsqrt(ms + EPS) * gm_ref[...].astype(jnp.float32).reshape(1, hid)).astype(jnp.bfloat16)
 
     def drain(i, carry):
         for cp in kv_out(i):
@@ -155,30 +188,32 @@
     vflat = vc.reshape(rows, keys, HEAD)
     vm = pl.BlockSpec(memory_space=pltpu.VMEM)
     hbm = pl.BlockSpec(memory_space=pl.ANY)
-    sm = pl.BlockSpec(memory_space=pltpu.SMEM)
     bf, f32 = jnp.bfloat16, jnp.float32
+    dma = pltpu.SemaphoreType.DMA
     hidden, m, ko, vo = pl.pallas_call(
         functools.partial(attn_kernel, rows=rows, blk=blk, heads=heads, groups=groups, qc=qc),
         name="attn",
-        out_shape=(jax.ShapeDtypeStruct((rows, hid), f32), jax.ShapeDtypeStruct((rows, hid), bf),
+        out_shape=(pltpu.VMEM((rows, hid), f32), pltpu.VMEM((rows, hid), bf),
                    jax.ShapeDtypeStruct(kflat.shape, bf), jax.ShapeDtypeStruct(vflat.shape, bf)),
-        in_specs=[sm, vm, vm, vm, hbm, vm, hbm, vm, hbm, hbm],
+        in_specs=[hbm] * 10,
         out_specs=(vm, vm, hbm, hbm),
         scratch_shapes=[
             pltpu.VMEM((rows, keys, HEAD), bf), pltpu.VMEM((rows, keys, HEAD), bf),
             pltpu.VMEM(wqkv.shape, bf), pltpu.VMEM(wproj.shape, bf),
+            pltpu.SMEM((rows,), jnp.int32), pltpu.VMEM((1, HEAD), f32), pltpu.VMEM((rows, hid), bf),
+            pltpu.VMEM(ga.shape, bf), pltpu.VMEM(bqkv.shape, bf), pltpu.VMEM(gm.shape, bf),
             pltpu.VMEM((rows, hid), bf), pltpu.VMEM((rows, HEAD), f32),
             pltpu.VMEM((rows * heads, HEAD), f32),
             pltpu.VMEM((rows * groups, HEAD), f32), pltpu.VMEM((rows * groups, HEAD), f32),
+            pltpu.VMEM((blk // 2, 2 * heads, keys), f32), pltpu.VMEM((blk // 2, 2 * heads, keys), bf),
             pltpu.VMEM((rows * heads, HEAD), f32), pltpu.VMEM((rows, heads * HEAD), bf),
-            pltpu.SemaphoreType.DMA((wqkv.shape[1] // qc,)), pltpu.SemaphoreType.DMA(()),
-            pltpu.SemaphoreType.DMA((nblk,)), pltpu.SemaphoreType.DMA((nblk,)),
-            pltpu.SemaphoreType.DMA((nblk,)), pltpu.SemaphoreType.DMA((nblk,)),
+            dma((6,)), dma((wqkv.shape[1] // qc,)), dma(()),
+            dma((nblk,)), dma((nblk,)), dma((nblk,)), dma((nblk,)),
         ],
         compiler_params=pltpu.CompilerParams(vmem_limit_bytes=60 * 1024 * 1024),
         cost_estimate=pl.CostEstimate(flops=2 * rows * hid * 4608 + 4 * rows * heads * keys * HEAD,
                                       bytes_accessed=86000000, transcendentals=rows * heads * keys),
-    )(lens, jnp.asarray(freq), x, ga.reshape(1, -1), wqkv, bqkv.reshape(1, -1), wproj, gm.reshape(1, -1), kflat, vflat)
+    )(lens, jnp.asarray(freq), x, ga, wqkv, bqkv, wproj, gm, kflat, vflat)
     return hidden, m, ko.reshape(kc.shape), vo.reshape(vc.shape)
 
 
@@ -351,9 +386,10 @@
             dma((chunks, 4)), dma((chunks, 8)), dma((chunks, 4)),
             dma((chunks, ncol)), dma((chunks, ncol)), dma((chunks, ncol, 3)), dma((chunks, ncol, 3)),
         ],
-        compiler_params=pltpu.CompilerParams(collective_id=0, has_side_effects=True, vmem_limit_bytes=60 * 1024 * 1024),
+        compiler_params=pltpu.CompilerParams(collective_id=0, has_side_effects=True, vmem_limit_bytes=34 << 20),
         cost_estimate=pl.CostEstimate(flops=2 * 8 * rows * hid * ffn * 3, bytes_accessed=17000000, transcendentals=8 * rows * ffn),
-    )(hidden, m, w_in, w_out)
+    )(pltpu.with_memory_space_constraint(hidden, pltpu.VMEM), pltpu.with_memory_space_constraint(m, pltpu.VMEM),
+      pltpu.with_memory_space_constraint(w_in, pltpu.HBM), pltpu.with_memory_space_constraint(w_out, pltpu.HBM))
 
 
 def solution(mesh):

time: 83.3 us -> 66.7 us (0.80)
  Pallas kernels: 76.9 us -> 65.2 us
  local copies, waits for them, and re-layouts: 5.53 us -> 0.71 us
    pallas_call x1, Pallas kernels: 36.3 us -> 26.4 us  [attention(): pl.pallas_call(functools.partial(attn_kernel, rows=rows, blk=blk, heads=h...]
    reshape x3 -> x0, local copies, waits for them, and re-layouts: 3.86 us -> none  [the longest x1 1.29 us: attention(): bqkv.reshape(1, -1)]
    pallas_call x1, Pallas kernels: 40.6 us -> 38.9 us  [mlp(): pl.pallas_call(functools.partial(mlp_kernel, chunks=chunks, crows=crows,...]
    unnamed x1, local copies, waits for them, and re-layouts: 1.67 us -> 0.71 us
where the time goes in v3:
time: 66.7 us; the launch traced here: 66.6 us
  Pallas kernels  65.2 us (98%)
  local copies, waits for them, and re-layouts  0.71 us (1%)
    pallas_call x1, Pallas kernels, mlp(): pl.pallas_call(functools.partial(mlp_kernel, chunks=chunks, crows=crows,...  38.9 us
    pallas_call x1, Pallas kernels, attention(): pl.pallas_call(functools.partial(attn_kernel, rows=rows, blk=blk, heads=h...  26.4 us

profile of v3, /device:TPU:0, one launch (start us, length us, event | category | flops | bytes accessed | tf_op | source)
XLA Modules:
  0.0 66.6 jit_solution(9707720948003843417)
XLA Ops:
  0.6 26.4 %attn.1 = (f32[64,2048]{1,0:T(8,128)S(1)}, bf16[64,2048]{1,0:T(8,128)(2,1)S(1)}, bf16[64,1024,128]{2,1,0:T(8,128)(2,1)}, bf16[64,1024,128]{2,1,0:T(8,128)(2,1)}) custom-call(s32[64]{0:T(128)} %len_hbm.1, f32[1,128]{1,0:T(1,128)} %constant.2.clone.freq_hbm, bf16[64,2048]{1,0:T(8,128)(2,1)} %x_hbm.1, bf16[2048]{0:T(1024)(128)(2,1)} %ga_hbm.1, ...), custom_call_target="tpu_custom_call" | custom-call | flops 1744830464 | bytes 86000000 | tf_op jit(solution)/shard_map/attn/pallas_call | solution.py:193
  27.0 38.9 %mlp.1 = bf16[64,2048]{1,0:T(8,128)(2,1)S(1)} custom-call(f32[64,2048]{1,0:T(8,128)S(1)} %get-tuple-element.7.hid_ref, bf16[64,2048]{1,0:T(8,128)(2,1)S(1)} %get-tuple-element.8.m_ref, bf16[2,1376,2048]{2,1,0:T(8,128)(2,1)} %wi_hbm.1, bf16[1376,2048]{1,0:T(8,128)(2,1)} %wo_hbm.1), custom_call_target="tpu_custom_call" | custom-call | flops 8657043456 | bytes 17000000 | tf_op jit(solution)/shard_map/mlp/pallas_call | solution.py:373
  65.9 0.7 %copy.16 = bf16[64,2048]{1,0:T(8,128)(2,1)} copy(bf16[64,2048]{1,0:T(8,128)(2,1)S(1)} %mlp.1) | data formatting | bytes 524288

commit v4 on v3

--- a/solution.py
+++ b/solution.py
@@ -218,175 +218,272 @@
 
 
 def mlp_kernel(hid_ref, m_ref, wi_hbm, wo_hbm, out_ref,
-               wi, wt, wo, gath, act, own_s, ps, rb, sb, rr,
-               wi_sem, wt_sem, wo_sem, ag_send, ag_recv, fw_send, ps_send, ps_recv, rs_send, rs_recv,
-               *, chunks, crows, full, tail, fc, nc):
-    hid = m_ref.shape[1]
+               wi, wt, wtr, wo, chip, gath, act, own_s, part_s, cps, crb, ps, rb, sb, t1, rr,
+               wi_sem, wt_sem, wo_sem, peer_send, peer_recv, near_send, near_recv, rel_send, rel_recv,
+               fw_send, fw_recv, cp_send, cp_recv, ps_send, ps_recv, rs_send, t1_recv, rr_recv,
+               *, chunks, full, tail, fc, nc):
+    rows, hid = m_ref.shape
+    crows = rows // chunks
+    half = crows // 2
     ncol = hid // nc
+    width = full * fc + fc // 2
+    bf, f32 = jnp.bfloat16, jnp.float32
     me = lax.axis_index('grp')
     core, xx, yy = me % 2, (me // 2) % 2, me // 4
     peer = me + 1 - 2 * core
-    near_x = me + 2 - 4 * xx
-    near_y = me + 4 - 8 * yy
-    diag = me + 2 - 4 * xx + 4 - 8 * yy
-    remote = (near_x, near_y, diag)
+    near = (me + 2 - 4 * xx, me + 4 - 8 * yy)
 
     def wi_copy(f, g):
         sl = pl.ds(f * fc, fc)
         return pltpu.make_async_copy(wi_hbm.at[g, sl], wi.at[g, sl], wi_sem.at[f, g])
 
     def wt_copy(g):
-        return pltpu.make_async_copy(wi_hbm.at[g, pl.ds(full * fc, tail)], wt.at[pl.ds(g * (fc // 2), tail)], wt_sem.at[g])
-
-    def wo_copy(c):
-        return pltpu.make_async_copy(wo_hbm.at[:, pl.ds(c * nc, nc)],
-                                     wo.at[pl.ds(0, full * fc + tail), pl.ds(c * nc, nc)], wo_sem.at[c])
+        return pltpu.make_async_copy(wi_hbm.at[g, pl.ds(full * fc, tail)], wt.at[g, pl.ds(0, tail)], wt_sem.at[g])
+
+    wo_copy = pltpu.make_async_copy(wo_hbm, wo.at[pl.ds(0, full * fc + tail)], wo_sem)
 
     for f in range(full):
         for g in range(2):
             wi_copy(f, g).start()
     for g in range(2):
         wt_copy(g).start()
-    for c in range(ncol):
-        wo_copy(c).start()
+    wo_copy.start()
 
     def rcopy(src, dst, ss, rs, dev):
         return pltpu.make_async_remote_copy(src_ref=src, dst_ref=dst, send_sem=ss, recv_sem=rs,
                                             device_id={'grp': dev}, device_id_type=pl.DeviceIdType.MESH)
 
-    def own_send(h, q):
-        slot, dev = ((4, peer), (1, near_x), (2, near_y), (3, diag))[q]
-        return rcopy(m_ref.at[pl.ds(h * crows, crows)], gath.at[h, pl.ds(slot * crows, crows)],
-                     ag_send.at[h, q], ag_recv.at[h, slot], dev)
-
-    def forward(h, q):
-        return rcopy(gath.at[h, pl.ds(q * crows, crows)], gath.at[h, pl.ds((q + 4) * crows, crows)],
-                     fw_send.at[h, q], ag_recv.at[h, q + 4], peer)
+    def g_at(h, slot, p=None):
+        if p is None:
+            return gath.at[h, pl.ds(slot * crows, crows)]
+        return gath.at[h, pl.ds(slot * crows + p * half, half)]
+
+    to_peer = rcopy(m_ref, chip.at[pl.ds(rows, rows)], peer_send, peer_recv, peer)
+
+    def to_near(h, d, p):
+        return rcopy(m_ref.at[pl.ds(h * crows + p * half, half)], g_at(h, d, p),
+                     near_send.at[h, d, p], near_recv.at[h, d, p], near[d])
+
+    def relay(h, d):
+        return rcopy(g_at(h, d, d), g_at(h, 2, d), rel_send.at[h, d], rel_recv.at[h, d], near[1 - d])
+
+    def forward(h, s):
+        return rcopy(g_at(h, s), g_at(h, 3 + s), fw_send.at[h, s], fw_recv.at[h, s], peer)
+
+    def cols(c):
+        return slice(c * nc, (c + 1) * nc)
+
+    def chip_send(c):
+        sl = (slice(None), pl.ds(c * nc, nc))
+        return rcopy(cps.at[sl], crb.at[sl], cp_send.at[c], cp_recv.at[c], peer)
 
     def pair_send(h, c):
         sl = (h, slice(None), pl.ds(c * nc, nc))
         return rcopy(ps.at[sl], rb.at[sl], ps_send.at[h, c], ps_recv.at[h, c], peer)
 
-    def part_send(h, c, q):
-        sl = (h, q, slice(None), pl.ds(c * nc, nc))
-        return rcopy(sb.at[sl], rr.at[sl], rs_send.at[h, c, q], rs_recv.at[h, c, q], remote[q])
+    def diag_send(h, c, d):
+        sl = (h, d, slice(None), pl.ds(c * nc, nc))
+        return rcopy(sb.at[sl], t1.at[sl], rs_send.at[h, c, d], t1_recv.at[h, c, d], near[d])
+
+    def near_part(h, c, d, p):
+        k = 2 + 2 * d + p
+        return rcopy(sb.at[h, k, :, pl.ds(c * nc, nc)], rr.at[h, d, p, :, pl.ds(c * nc, nc)],
+                     rs_send.at[h, c, k], rr_recv.at[h, c, d, p], near[d])
 
     barrier = pltpu.get_barrier_semaphore()
-    for dev in (peer,) + remote:
+    for dev in (peer,) + near:
         pl.semaphore_signal(barrier, inc=1, device_id={'grp': dev}, device_id_type=pl.DeviceIdType.MESH)
-    pl.semaphore_wait(barrier, 4)
-
+    pl.semaphore_wait(barrier, 3)
+
+    def send_own(h):
+        for p in range(2):
+            for d in range(2):
+                to_near(h, d, p if d == 0 else 1 - p).start()
+
+    def pass_on(h):
+        for d in range(2):
+            to_near(h, d, d).wait_recv()
+            relay(h, d).start()
+
+    def share(h):
+        for d in range(2):
+            to_near(h, d, 1 - d).wait_recv()
+            forward(h, d).start()
+
+    def share_diag(h):
+        for d in range(2):
+            relay(h, d).wait_recv()
+        forward(h, 2).start()
+
+    def all_here(h):
+        for s in range(3):
+            forward(h, s).wait_recv()
+
+    to_peer.start()
+    send_own(0)
+    for g in range(2):
+        wt[g, tail:, :] = jnp.zeros((fc // 2 - tail, hid), bf)
+    wo[full * fc + tail:, :] = jnp.zeros((fc // 2 - tail, hid), bf)
+    chip[0:rows] = m_ref[...]
+    to_peer.wait_recv()
+
+    def gated(gate, up):
+        return (jax.nn.silu(gate) * up).astype(bf)
+
+    nt = (((1,), (1,)), ((), ()))
+    for f in range(full + 1):
+        n = fc if f < full else fc // 2
+        sl = slice(f * fc, f * fc + n)
+        for g in range(2):
+            (wi_copy(f, g) if f < full else wt_copy(g)).wait()
+        raw = [wi[g, sl, :] if f < full else wt[g] for g in range(2)]
+        gu = [lax.dot_general(chip[...], w, nt, preferred_element_type=f32) for w in raw]
+        for g in range(2):
+            wtr[g, :, sl] = raw[g].T
+        act[0:2 * rows, sl] = gated(gu[0], gu[1])
+        if f == HOOK_PASS:
+            pass_on(0)
+            send_own(1)
+        if f == HOOK_SHARE:
+            share(0)
+    wo_copy.wait()
+    for c in range(ncol):
+        part = jnp.dot(act[0:2 * rows, :], wo[:, cols(c)], preferred_element_type=f32)
+        cps[:, cols(c)] = part[rows:].astype(bf)
+        own_s[:, cols(c)] = part[:rows]
+        chip_send(c).start()
+
+    def in_proj(h):
+        for lo, hi in IN_CUTS:
+            gate = jnp.dot(gath[h], wtr[0, :, lo:hi], preferred_element_type=f32)
+            up = jnp.dot(gath[h], wtr[1, :, lo:hi], preferred_element_type=f32)
+            act[0:6 * crows, lo:hi] = gated(gate, up)
+
+    def out_proj(h):
+        for c in range(ncol):
+            part = jnp.dot(act[0:6 * crows, :], wo[:, cols(c)], preferred_element_type=f32)
+            ps[h, :, cols(c)] = part[3 * crows:].astype(bf)
+            part_s[h, :, cols(c)] = part[:3 * crows]
+            pair_send(h, c).start()
+
+    def stage1(h, c):
+        pair_send(h, c).wait_recv()
+        tot = part_s[h, :, cols(c)] + rb[h, :, cols(c)].astype(f32)
+        part_s[h, 0:2 * crows, cols(c)] = tot[0:2 * crows]
+        for d in range(2):
+            r = 2 * crows + d * half
+            sb[h, d, :, cols(c)] = tot[r:r + half].astype(bf)
+            r = d * crows + d * half
+            sb[h, 2 + 2 * d + d, :, cols(c)] = tot[r:r + half].astype(bf)
+        for d in range(2):
+            diag_send(h, c, d).start()
+        for d in range(2):
+            near_part(h, c, d, d).start()
+
+    def stage2(h, c):
+        for d in range(2):
+            e = 1 - d
+            diag_send(h, c, d).wait_recv()
+            r = e * crows + d * half
+            sb[h, 2 + 2 * e + d, :, cols(c)] = (part_s[h, r:r + half, cols(c)] + t1[h, d, :, cols(c)].astype(f32)).astype(bf)
+            near_part(h, c, e, d).start()
+
+    def chip_sum(c):
+        chip_send(c).wait_recv()
+        own_s[:, cols(c)] = hid_ref[:, cols(c)] + own_s[:, cols(c)] + crb[:, cols(c)].astype(f32)
+
+    def finish(h, c):
+        for d in range(2):
+            for p in range(2):
+                near_part(h, c, d, p).wait_recv()
+        rs = slice(h * crows, (h + 1) * crows)
+        tot = own_s[rs, cols(c)]
+        for d in range(2):
+            tot = tot + rr[h, d, :, :, cols(c)].reshape(crows, nc).astype(f32)
+        out_ref[rs, cols(c)] = tot.astype(bf)
+
+    share_diag(0)
+    pass_on(1)
+    for c in range(ncol):
+        chip_sum(c)
+    all_here(0)
+    in_proj(0)
+    share(1)
+    out_proj(0)
+    share_diag(1)
+    for c in range(ncol):
+        stage1(0, c)
+    all_here(1)
+    in_proj(1)
+    out_proj(1)
+    for c in range(ncol):
+        stage2(0, c)
+    for c in range(ncol):
+        stage1(1, c)
+    for c in range(ncol):
+        finish(0, c)
+    for c in range(ncol):
+        stage2(1, c)
+    for c in range(ncol):
+        finish(1, c)
+
+    to_peer.wait_send()
+    for c in range(ncol):
+        chip_send(c).wait_send()
     for h in range(chunks):
-        for q in (1, 2, 3, 0):
-            own_send(h, q).start()
-
-    pad = fc // 2 - tail
-    for g in range(2):
-        wt[g * (fc // 2) + tail:(g + 1) * (fc // 2), :] = jnp.zeros((pad, hid), jnp.bfloat16)
-    wo[full * fc + tail:, :] = jnp.zeros((pad, hid), jnp.bfloat16)
-    for h in range(chunks):
-        gath[h, 0:crows] = m_ref[h * crows:(h + 1) * crows, :]
-
-    nt = (((1,), (1,)), ((), ()))
-
-    def pair_sum(h, c):
-        pair_send(h, c).wait_recv()
-        cs = slice(c * nc, (c + 1) * nc)
-        tot = own_s[h, :, cs] + rb[h, :, cs].astype(jnp.float32)
-        own_s[h, 0:crows, cs] = tot[0:crows]
-        for q in range(3):
-            sb[h, q, :, cs] = tot[(q + 1) * crows:(q + 2) * crows].astype(jnp.bfloat16)
-        for q in (2, 0, 1):
-            part_send(h, c, q).start()
-
-    for h in range(chunks):
-        for q in (1, 2, 3):
-            own_send(h, q).wait_recv()
-            forward(h, q).start()
-        own_send(h, 0).wait_recv()
-        for q in (1, 2, 3):
-            forward(h, q).wait_recv()
-
-        def in_proj(f, carry):
-            if h == 0:
-                for g in range(2):
-                    wi_copy(f, g).wait()
-            sl = pl.ds(pl.multiple_of(f * fc, fc), fc)
-            gate = lax.dot_general(gath[h], wi[0, sl, :], nt, preferred_element_type=jnp.float32)
-            up = lax.dot_general(gath[h], wi[1, sl, :], nt, preferred_element_type=jnp.float32)
-            act[:, sl] = (jax.nn.silu(gate) * up).astype(jnp.bfloat16)
-            return carry
-
-        lax.fori_loop(0, full, in_proj, 0)
-        if h == 0:
-            for g in range(2):
-                wt_copy(g).wait()
-        gu = lax.dot_general(gath[h], wt[...], nt, preferred_element_type=jnp.float32)
-        act[:, full * fc:] = (jax.nn.silu(gu[:, :fc // 2]) * gu[:, fc // 2:]).astype(jnp.bfloat16)
-
-        half = 4 * crows
-        for c in range(ncol):
-            if h == 0:
-                wo_copy(c).wait()
-            cs = slice(c * nc, (c + 1) * nc)
-            part = jnp.dot(act[...], wo[:, cs], preferred_element_type=jnp.float32)
-            ps[h, :, cs] = part[half:].astype(jnp.bfloat16)
-            own_s[h, :, cs] = part[:half]
-            pair_send(h, c).start()
-            if c > 0:
-                pair_sum(h, c - 1)
-        pair_sum(h, ncol - 1)
-
-    for h in range(chunks):
-        rs = slice(h * crows, (h + 1) * crows)
-        for c in range(ncol):
-            cs = slice(c * nc, (c + 1) * nc)
-            for q in range(3):
-                part_send(h, c, q).wait_recv()
-            tot = hid_ref[rs, cs] + own_s[h, 0:crows, cs]
-            for q in range(3):
-                tot = tot + rr[h, q, :, cs].astype(jnp.float32)
-            out_ref[rs, cs] = tot.astype(jnp.bfloat16)
-
-    for h in range(chunks):
-        for q in range(4):
-            own_send(h, q).wait_send()
-        for q in (1, 2, 3):
-            forward(h, q).wait_send()
+        for d in range(2):
+            for p in range(2):
+                to_near(h, d, p).wait_send()
+            relay(h, d).wait_send()
+        for s in range(3):
+            forward(h, s).wait_send()
         for c in range(ncol):
             pair_send(h, c).wait_send()
-            for q in range(3):
-                part_send(h, c, q).wait_send()
+            for d in range(2):
+                diag_send(h, c, d).wait_send()
+                for p in range(2):
+                    near_part(h, c, d, p).wait_send()
+
+
+HOOK_PASS = 2
+HOOK_SHARE = 5
+IN_CUTS = ((0, 512), (512, 1024), (1024, 1408))
 
 
 def mlp(hidden, m, w_in, w_out):
     rows, hid = m.shape
     ffn = w_out.shape[0]
-    chunks, fc, nc = 2, 256, 512
+    chunks, fc, nc = 2, 256, 1024
     crows = rows // chunks
+    half = crows // 2
     full, tail = ffn // fc, ffn % fc
+    width = full * fc + fc // 2
     ncol = hid // nc
     vm = pl.BlockSpec(memory_space=pltpu.VMEM)
     hbm = pl.BlockSpec(memory_space=pl.ANY)
     bf, f32 = jnp.bfloat16, jnp.float32
     dma = pltpu.SemaphoreType.DMA
     return pl.pallas_call(
-        functools.partial(mlp_kernel, chunks=chunks, crows=crows, full=full, tail=tail, fc=fc, nc=nc),
+        functools.partial(mlp_kernel, chunks=chunks, full=full, tail=tail, fc=fc, nc=nc),
         name="mlp",
         out_shape=jax.ShapeDtypeStruct((rows, hid), bf),
         in_specs=[vm, vm, hbm, hbm],
         out_specs=vm,
         scratch_shapes=[
-            pltpu.VMEM((2, full * fc, hid), bf), pltpu.VMEM((fc, hid), bf), pltpu.VMEM((full * fc + fc // 2, hid), bf),
-            pltpu.VMEM((chunks, 8 * crows, hid), bf), pltpu.VMEM((8 * crows, full * fc + fc // 2), bf),
-            pltpu.VMEM((chunks, 4 * crows, hid), f32), pltpu.VMEM((chunks, 4 * crows, hid), bf),
-            pltpu.VMEM((chunks, 4 * crows, hid), bf),
-            pltpu.VMEM((chunks, 3, crows, hid), bf), pltpu.VMEM((chunks, 3, crows, hid), bf),
-            dma((full, 2)), dma((2,)), dma((ncol,)),
-            dma((chunks, 4)), dma((chunks, 8)), dma((chunks, 4)),
-            dma((chunks, ncol)), dma((chunks, ncol)), dma((chunks, ncol, 3)), dma((chunks, ncol, 3)),
+            pltpu.VMEM((2, full * fc, hid), bf), pltpu.VMEM((2, fc // 2, hid), bf), pltpu.VMEM((2, hid, width), bf),
+            pltpu.VMEM((width, hid), bf),
+            pltpu.VMEM((2 * rows, hid), bf), pltpu.VMEM((chunks, 6 * crows, hid), bf), pltpu.VMEM((6 * crows, width), bf),
+            pltpu.VMEM((rows, hid), f32), pltpu.VMEM((chunks, 3 * crows, hid), f32),
+            pltpu.VMEM((rows, hid), bf), pltpu.VMEM((rows, hid), bf),
+            pltpu.VMEM((chunks, 3 * crows, hid), bf), pltpu.VMEM((chunks, 3 * crows, hid), bf),
+            pltpu.VMEM((chunks, 6, half, hid), bf), pltpu.VMEM((chunks, 2, half, hid), bf),
+            pltpu.VMEM((chunks, 2, 2, half, hid), bf),
+            dma((full, 2)), dma((2,)), dma(()),
+            dma(()), dma(()), dma((chunks, 2, 2)), dma((chunks, 2, 2)), dma((chunks, 2)), dma((chunks, 2)),
+            dma((chunks, 3)), dma((chunks, 3)), dma((ncol,)), dma((ncol,)), dma((chunks, ncol)), dma((chunks, ncol)),
+            dma((chunks, ncol, 6)), dma((chunks, ncol, 2)), dma((chunks, ncol, 2, 2)),
         ],
-        compiler_params=pltpu.CompilerParams(collective_id=0, has_side_effects=True, vmem_limit_bytes=34 << 20),
+        compiler_params=pltpu.CompilerParams(collective_id=0, has_side_effects=True, vmem_limit_bytes=46 << 20),
         cost_estimate=pl.CostEstimate(flops=2 * 8 * rows * hid * ffn * 3, bytes_accessed=17000000, transcendentals=8 * rows * ffn),
     )(pltpu.with_memory_space_constraint(hidden, pltpu.VMEM), pltpu.with_memory_space_constraint(m, pltpu.VMEM),
       pltpu.with_memory_space_constraint(w_in, pltpu.HBM), pltpu.with_memory_space_constraint(w_out, pltpu.HBM))

time: 66.7 us -> 60.1 us (0.901)
  Pallas kernels: 65.2 us -> 58.7 us
    pallas_call x1, Pallas kernels: 38.9 us -> 32.3 us  [mlp(): pl.pallas_call(functools.partial(mlp_kernel, chunks=chunks, full=full, ta...]
where the time goes in v4:
time: 60.1 us
  Pallas kernels  58.7 us (98%)
  local copies, waits for them, and re-layouts  0.71 us (1%)
  between operations  0.65 us (1%)
    pallas_call x1, Pallas kernels, mlp(): pl.pallas_call(functools.partial(mlp_kernel, chunks=chunks, full=full, ta...  32.3 us
    pallas_call x1, Pallas kernels, attention(): pl.pallas_call(functools.partial(attn_kernel, rows=rows, blk=blk, heads=h...  26.4 us

profile of v4, /device:TPU:0, one launch (start us, length us, event | category | flops | bytes accessed | tf_op | source)
XLA Modules:
  0.0 60.1 jit_solution(15775347036383636578)
XLA Ops:
  0.6 26.4 %attn.1 = (f32[64,2048]{1,0:T(8,128)S(1)}, bf16[64,2048]{1,0:T(8,128)(2,1)S(1)}, bf16[64,1024,128]{2,1,0:T(8,128)(2,1)}, bf16[64,1024,128]{2,1,0:T(8,128)(2,1)}) custom-call(s32[64]{0:T(128)} %len_hbm.1, f32[1,128]{1,0:T(1,128)} %constant.2.clone.freq_hbm, bf16[64,2048]{1,0:T(8,128)(2,1)} %x_hbm.1, bf16[2048]{0:T(1024)(128)(2,1)} %ga_hbm.1, ...), custom_call_target="tpu_custom_call" | custom-call | flops 1744830464 | bytes 86000000 | tf_op jit(solution)/shard_map/attn/pallas_call | solution.py:193
  27.0 32.3 %mlp.1 = bf16[64,2048]{1,0:T(8,128)(2,1)S(1)} custom-call(f32[64,2048]{1,0:T(8,128)S(1)} %get-tuple-element.7.hid_ref, bf16[64,2048]{1,0:T(8,128)(2,1)S(1)} %get-tuple-element.8.m_ref, bf16[2,1376,2048]{2,1,0:T(8,128)(2,1)} %wi_hbm.1, bf16[1376,2048]{1,0:T(8,128)(2,1)} %wo_hbm.1), custom_call_target="tpu_custom_call" | custom-call | flops 8657043456 | bytes 17000000 | tf_op jit(solution)/shard_map/mlp/pallas_call | solution.py:466
  59.3 0.7 %copy.16 = bf16[64,2048]{1,0:T(8,128)(2,1)} copy(bf16[64,2048]{1,0:T(8,128)(2,1)S(1)} %mlp.1) | data formatting | bytes 524288

commit v5 on v4

--- a/solution.py
+++ b/solution.py
@@ -221,12 +221,10 @@
                wi, wt, wtr, wo, chip, gath, act, own_s, part_s, cps, crb, ps, rb, sb, t1, rr,
                wi_sem, wt_sem, wo_sem, peer_send, peer_recv, near_send, near_recv, rel_send, rel_recv,
                fw_send, fw_recv, cp_send, cp_recv, ps_send, ps_recv, rs_send, t1_recv, rr_recv,
-               *, chunks, full, tail, fc, nc):
+               *, sizes, full, tail, fc, nc):
     rows, hid = m_ref.shape
-    crows = rows // chunks
-    half = crows // 2
     ncol = hid // nc
-    width = full * fc + fc // 2
+    first = [sum(sizes[:h]) for h in range(len(sizes))]
     bf, f32 = jnp.bfloat16, jnp.float32
     me = lax.axis_index('grp')
     core, xx, yy = me % 2, (me // 2) % 2, me // 4
@@ -253,52 +251,55 @@
         return pltpu.make_async_remote_copy(src_ref=src, dst_ref=dst, send_sem=ss, recv_sem=rs,
                                             device_id={'grp': dev}, device_id_type=pl.DeviceIdType.MESH)
 
-    def g_at(h, slot, p=None):
-        if p is None:
-            return gath.at[h, pl.ds(slot * crows, crows)]
-        return gath.at[h, pl.ds(slot * crows + p * half, half)]
+    def cols(c):
+        return slice(c * nc, (c + 1) * nc)
+
+    def g_at(h, slot, c=None):
+        sl = pl.ds(6 * first[h] + slot * sizes[h], sizes[h])
+        return gath.at[sl] if c is None else gath.at[sl, pl.ds(c * nc, nc)]
 
     to_peer = rcopy(m_ref, chip.at[pl.ds(rows, rows)], peer_send, peer_recv, peer)
 
-    def to_near(h, d, p):
-        return rcopy(m_ref.at[pl.ds(h * crows + p * half, half)], g_at(h, d, p),
-                     near_send.at[h, d, p], near_recv.at[h, d, p], near[d])
+    def to_near(h, d, c):
+        return rcopy(m_ref.at[pl.ds(first[h], sizes[h]), pl.ds(c * nc, nc)], g_at(h, d, c),
+                     near_send.at[h, d, c], near_recv.at[h, d, c], near[d])
 
     def relay(h, d):
         return rcopy(g_at(h, d, d), g_at(h, 2, d), rel_send.at[h, d], rel_recv.at[h, d], near[1 - d])
 
     def forward(h, s):
         return rcopy(g_at(h, s), g_at(h, 3 + s), fw_send.at[h, s], fw_recv.at[h, s], peer)
-
-    def cols(c):
-        return slice(c * nc, (c + 1) * nc)
 
     def chip_send(c):
         sl = (slice(None), pl.ds(c * nc, nc))
         return rcopy(cps.at[sl], crb.at[sl], cp_send.at[c], cp_recv.at[c], peer)
 
     def pair_send(h, c):
-        sl = (h, slice(None), pl.ds(c * nc, nc))
+        sl = (pl.ds(3 * first[h], 3 * sizes[h]), pl.ds(c * nc, nc))
         return rcopy(ps.at[sl], rb.at[sl], ps_send.at[h, c], ps_recv.at[h, c], peer)
 
-    def diag_send(h, c, d):
-        sl = (h, d, slice(None), pl.ds(c * nc, nc))
-        return rcopy(sb.at[sl], t1.at[sl], rs_send.at[h, c, d], t1_recv.at[h, c, d], near[d])
-
-    def near_part(h, c, d, p):
-        k = 2 + 2 * d + p
-        return rcopy(sb.at[h, k, :, pl.ds(c * nc, nc)], rr.at[h, d, p, :, pl.ds(c * nc, nc)],
-                     rs_send.at[h, c, k], rr_recv.at[h, c, d, p], near[d])
+    def sb_at(h, k):
+        return slice(3 * first[h] + k * sizes[h], 3 * first[h] + (k + 1) * sizes[h])
+
+    def rows_of(h):
+        return slice(first[h], first[h] + sizes[h])
+
+    def diag_send(h, c):
+        return rcopy(sb.at[sb_at(h, 2), pl.ds(c * nc, nc)], t1.at[rows_of(h), pl.ds(c * nc, nc)],
+                     rs_send.at[h, c, 2], t1_recv.at[h, c], near[c])
+
+    def near_part(h, c, d):
+        return rcopy(sb.at[sb_at(h, d), pl.ds(c * nc, nc)], rr.at[d, rows_of(h), pl.ds(c * nc, nc)],
+                     rs_send.at[h, c, d], rr_recv.at[h, c, d], near[d])
 
     barrier = pltpu.get_barrier_semaphore()
     for dev in (peer,) + near:
         pl.semaphore_signal(barrier, inc=1, device_id={'grp': dev}, device_id_type=pl.DeviceIdType.MESH)
     pl.semaphore_wait(barrier, 3)
 
-    def send_own(h):
-        for p in range(2):
-            for d in range(2):
-                to_near(h, d, p if d == 0 else 1 - p).start()
+    def send_half(h, k):
+        for d in range(2):
+            to_near(h, d, k if d == 0 else 1 - k).start()
 
     def pass_on(h):
         for d in range(2):
@@ -320,142 +321,137 @@
             forward(h, s).wait_recv()
 
     to_peer.start()
-    send_own(0)
+    send_half(0, 0)
+    send_half(0, 1)
+    send_half(1, 0)
     for g in range(2):
         wt[g, tail:, :] = jnp.zeros((fc // 2 - tail, hid), bf)
     wo[full * fc + tail:, :] = jnp.zeros((fc // 2 - tail, hid), bf)
     chip[0:rows] = m_ref[...]
-    to_peer.wait_recv()
 
     def gated(gate, up):
         return (jax.nn.silu(gate) * up).astype(bf)
 
-    nt = (((1,), (1,)), ((), ()))
     for f in range(full + 1):
         n = fc if f < full else fc // 2
         sl = slice(f * fc, f * fc + n)
         for g in range(2):
             (wi_copy(f, g) if f < full else wt_copy(g)).wait()
-        raw = [wi[g, sl, :] if f < full else wt[g] for g in range(2)]
-        gu = [lax.dot_general(chip[...], w, nt, preferred_element_type=f32) for w in raw]
-        for g in range(2):
-            wtr[g, :, sl] = raw[g].T
-        act[0:2 * rows, sl] = gated(gu[0], gu[1])
-        if f == HOOK_PASS:
+            wtr[g, :, sl] = (wi[g, sl, :] if f < full else wt[g]).T
+        if f == HOOK:
             pass_on(0)
-            send_own(1)
-        if f == HOOK_SHARE:
+            send_half(1, 1)
             share(0)
-    wo_copy.wait()
-    for c in range(ncol):
-        part = jnp.dot(act[0:2 * rows, :], wo[:, cols(c)], preferred_element_type=f32)
-        cps[:, cols(c)] = part[rows:].astype(bf)
-        own_s[:, cols(c)] = part[:rows]
-        chip_send(c).start()
+
+    def up_and_gate(g, n):
+        for lo, hi in IN_CUTS:
+            gate = jnp.dot(g, wtr[0, :, lo:hi], preferred_element_type=f32)
+            up = jnp.dot(g, wtr[1, :, lo:hi], preferred_element_type=f32)
+            act[0:n, lo:hi] = gated(gate, up)
+
+    def own_rows():
+        to_peer.wait_recv()
+        up_and_gate(chip[...], 2 * rows)
+        for c in range(ncol):
+            part = jnp.dot(act[0:2 * rows, :], wo[:, cols(c)], preferred_element_type=f32)
+            cps[:, cols(c)] = part[rows:].astype(bf)
+            own_s[:, cols(c)] = part[:rows]
+            chip_send(c).start()
 
     def in_proj(h):
-        for lo, hi in IN_CUTS:
-            gate = jnp.dot(gath[h], wtr[0, :, lo:hi], preferred_element_type=f32)
-            up = jnp.dot(gath[h], wtr[1, :, lo:hi], preferred_element_type=f32)
-            act[0:6 * crows, lo:hi] = gated(gate, up)
+        n = 6 * sizes[h]
+        up_and_gate(gath[6 * first[h]:6 * first[h] + n, :], n)
 
     def out_proj(h):
+        n = 3 * sizes[h]
+        sl = slice(3 * first[h], 3 * first[h] + n)
         for c in range(ncol):
-            part = jnp.dot(act[0:6 * crows, :], wo[:, cols(c)], preferred_element_type=f32)
-            ps[h, :, cols(c)] = part[3 * crows:].astype(bf)
-            part_s[h, :, cols(c)] = part[:3 * crows]
+            part = jnp.dot(act[0:2 * n, :], wo[:, cols(c)], preferred_element_type=f32)
+            ps[sl, cols(c)] = part[n:].astype(bf)
+            part_s[sl, cols(c)] = part[:n]
             pair_send(h, c).start()
 
-    def stage1(h, c):
-        pair_send(h, c).wait_recv()
-        tot = part_s[h, :, cols(c)] + rb[h, :, cols(c)].astype(f32)
-        part_s[h, 0:2 * crows, cols(c)] = tot[0:2 * crows]
-        for d in range(2):
-            r = 2 * crows + d * half
-            sb[h, d, :, cols(c)] = tot[r:r + half].astype(bf)
-            r = d * crows + d * half
-            sb[h, 2 + 2 * d + d, :, cols(c)] = tot[r:r + half].astype(bf)
-        for d in range(2):
-            diag_send(h, c, d).start()
-        for d in range(2):
-            near_part(h, c, d, d).start()
-
-    def stage2(h, c):
-        for d in range(2):
-            e = 1 - d
-            diag_send(h, c, d).wait_recv()
-            r = e * crows + d * half
-            sb[h, 2 + 2 * e + d, :, cols(c)] = (part_s[h, r:r + half, cols(c)] + t1[h, d, :, cols(c)].astype(f32)).astype(bf)
-            near_part(h, c, e, d).start()
+    def stage1(h):
+        for c in range(ncol):
+            pair_send(h, c).wait_recv()
+            e, n = 1 - c, sizes[h]
+            sl = slice(3 * first[h], 3 * first[h] + 3 * n)
+            tot = part_s[sl, cols(c)] + rb[sl, cols(c)].astype(f32)
+            part_s[sb_at(h, e), cols(c)] = tot[e * n:(e + 1) * n]
+            sb[sb_at(h, 2), cols(c)] = tot[2 * n:].astype(bf)
+            sb[sb_at(h, c), cols(c)] = tot[c * n:(c + 1) * n].astype(bf)
+            diag_send(h, c).start()
+            near_part(h, c, c).start()
+
+    def stage2(h):
+        for c in range(ncol):
+            e = 1 - c
+            diag_send(h, c).wait_recv()
+            sb[sb_at(h, e), cols(c)] = (part_s[sb_at(h, e), cols(c)] + t1[rows_of(h), cols(c)].astype(f32)).astype(bf)
+            near_part(h, c, e).start()
 
     def chip_sum(c):
         chip_send(c).wait_recv()
         own_s[:, cols(c)] = hid_ref[:, cols(c)] + own_s[:, cols(c)] + crb[:, cols(c)].astype(f32)
 
-    def finish(h, c):
-        for d in range(2):
-            for p in range(2):
-                near_part(h, c, d, p).wait_recv()
-        rs = slice(h * crows, (h + 1) * crows)
-        tot = own_s[rs, cols(c)]
-        for d in range(2):
-            tot = tot + rr[h, d, :, :, cols(c)].reshape(crows, nc).astype(f32)
-        out_ref[rs, cols(c)] = tot.astype(bf)
+    def finish(h):
+        for c in range(ncol):
+            for d in range(2):
+                near_part(h, c, d).wait_recv()
+            tot = own_s[rows_of(h), cols(c)]
+            for d in range(2):
+                tot = tot + rr[d, rows_of(h), cols(c)].astype(f32)
+            out_ref[rows_of(h), cols(c)] = tot.astype(bf)
 
     share_diag(0)
     pass_on(1)
-    for c in range(ncol):
-        chip_sum(c)
+    wo_copy.wait()
     all_here(0)
     in_proj(0)
     share(1)
     out_proj(0)
     share_diag(1)
-    for c in range(ncol):
-        stage1(0, c)
+    stage1(0)
     all_here(1)
     in_proj(1)
     out_proj(1)
+    stage2(0)
+    stage1(1)
+    own_rows()
+    stage2(1)
     for c in range(ncol):
-        stage2(0, c)
-    for c in range(ncol):
-        stage1(1, c)
-    for c in range(ncol):
-        finish(0, c)
-    for c in range(ncol):
-        stage2(1, c)
-    for c in range(ncol):
-        finish(1, c)
+        chip_sum(c)
+    finish(0)
+    finish(1)
 
     to_peer.wait_send()
     for c in range(ncol):
         chip_send(c).wait_send()
-    for h in range(chunks):
+    for h in range(len(sizes)):
         for d in range(2):
-            for p in range(2):
-                to_near(h, d, p).wait_send()
+            for c in range(2):
+                to_near(h, d, c).wait_send()
             relay(h, d).wait_send()
         for s in range(3):
             forward(h, s).wait_send()
         for c in range(ncol):
             pair_send(h, c).wait_send()
+            diag_send(h, c).wait_send()
             for d in range(2):
-                diag_send(h, c, d).wait_send()
-                for p in range(2):
-                    near_part(h, c, d, p).wait_send()
-
-
-HOOK_PASS = 2
-HOOK_SHARE = 5
+                near_part(h, c, d).wait_send()
+
+
+HOOK = 5
+SIZES = (32, 32)
 IN_CUTS = ((0, 512), (512, 1024), (1024, 1408))
 
 
 def mlp(hidden, m, w_in, w_out):
     rows, hid = m.shape
     ffn = w_out.shape[0]
-    chunks, fc, nc = 2, 256, 1024
-    crows = rows // chunks
-    half = crows // 2
+    fc, nc = 256, hid // 2
+    sizes = SIZES
+    chunks = len(sizes)
     full, tail = ffn // fc, ffn % fc
     width = full * fc + fc // 2
     ncol = hid // nc
@@ -464,24 +460,24 @@
     bf, f32 = jnp.bfloat16, jnp.float32
     dma = pltpu.SemaphoreType.DMA
     return pl.pallas_call(
-        functools.partial(mlp_kernel, chunks=chunks, full=full, tail=tail, fc=fc, nc=nc),
+        functools.partial(mlp_kernel, sizes=sizes, full=full, tail=tail, fc=fc, nc=nc),
         name="mlp",
-        out_shape=jax.ShapeDtypeStruct((rows, hid), bf),
+        out_shape=pltpu.VMEM((rows, hid), bf),
         in_specs=[vm, vm, hbm, hbm],
         out_specs=vm,
         scratch_shapes=[
             pltpu.VMEM((2, full * fc, hid), bf), pltpu.VMEM((2, fc // 2, hid), bf), pltpu.VMEM((2, hid, width), bf),
             pltpu.VMEM((width, hid), bf),
-            pltpu.VMEM((2 * rows, hid), bf), pltpu.VMEM((chunks, 6 * crows, hid), bf), pltpu.VMEM((6 * crows, width), bf),
-            pltpu.VMEM((rows, hid), f32), pltpu.VMEM((chunks, 3 * crows, hid), f32),
+            pltpu.VMEM((2 * rows, hid), bf), pltpu.VMEM((6 * rows, hid), bf),
+            pltpu.VMEM((max(2 * rows, 6 * max(sizes)), width), bf),
+            pltpu.VMEM((rows, hid), f32), pltpu.VMEM((3 * rows, hid), f32),
             pltpu.VMEM((rows, hid), bf), pltpu.VMEM((rows, hid), bf),
-            pltpu.VMEM((chunks, 3 * crows, hid), bf), pltpu.VMEM((chunks, 3 * crows, hid), bf),
-            pltpu.VMEM((chunks, 6, half, hid), bf), pltpu.VMEM((chunks, 2, half, hid), bf),
-            pltpu.VMEM((chunks, 2, 2, half, hid), bf),
+            pltpu.VMEM((3 * rows, hid), bf), pltpu.VMEM((3 * rows, hid), bf),
+            pltpu.VMEM((3 * rows, hid), bf), pltpu.VMEM((rows, hid), bf), pltpu.VMEM((2, rows, hid), bf),
             dma((full, 2)), dma((2,)), dma(()),
             dma(()), dma(()), dma((chunks, 2, 2)), dma((chunks, 2, 2)), dma((chunks, 2)), dma((chunks, 2)),
             dma((chunks, 3)), dma((chunks, 3)), dma((ncol,)), dma((ncol,)), dma((chunks, ncol)), dma((chunks, ncol)),
-            dma((chunks, ncol, 6)), dma((chunks, ncol, 2)), dma((chunks, ncol, 2, 2)),
+            dma((chunks, ncol, 3)), dma((chunks, ncol)), dma((chunks, ncol, 2)),
         ],
         compiler_params=pltpu.CompilerParams(collective_id=0, has_side_effects=True, vmem_limit_bytes=46 << 20),
         cost_estimate=pl.CostEstimate(flops=2 * 8 * rows * hid * ffn * 3, bytes_accessed=17000000, transcendentals=8 * rows * ffn),

time: 60.1 us -> 59.6 us (level)
  no operation moved by 1% of the time
where the time goes in v5:
time: 59.6 us; the launch traced here: 59.5 us
  Pallas kernels  58.1 us (97%)
  local copies, waits for them, and re-layouts  0.71 us (1%)
  between operations  0.65 us (1%)
    pallas_call x1, Pallas kernels, mlp(): pl.pallas_call(functools.partial(mlp_kernel, sizes=sizes, full=full, tail...  31.8 us
    pallas_call x1, Pallas kernels, attention(): pl.pallas_call(functools.partial(attn_kernel, rows=rows, blk=blk, heads=h...  26.4 us

profile of v5, /device:TPU:0, one launch (start us, length us, event | category | flops | bytes accessed | tf_op | source)
XLA Modules:
  0.0 59.5 jit_solution(10210131702581171487)
XLA Ops:
  0.6 26.4 %attn.1 = (f32[64,2048]{1,0:T(8,128)S(1)}, bf16[64,2048]{1,0:T(8,128)(2,1)S(1)}, bf16[64,1024,128]{2,1,0:T(8,128)(2,1)}, bf16[64,1024,128]{2,1,0:T(8,128)(2,1)}) custom-call(s32[64]{0:T(128)} %len_hbm.1, f32[1,128]{1,0:T(1,128)} %constant.2.clone.freq_hbm, bf16[64,2048]{1,0:T(8,128)(2,1)} %x_hbm.1, bf16[2048]{0:T(1024)(128)(2,1)} %ga_hbm.1, ...), custom_call_target="tpu_custom_call" | custom-call | flops 1744830464 | bytes 86000000 | tf_op jit(solution)/shard_map/attn/pallas_call | solution.py:193
  27.0 31.8 %mlp.1 = bf16[64,2048]{1,0:T(8,128)(2,1)S(1)} custom-call(f32[64,2048]{1,0:T(8,128)S(1)} %get-tuple-element.7.hid_ref, bf16[64,2048]{1,0:T(8,128)(2,1)S(1)} %get-tuple-element.8.m_ref, bf16[2,1376,2048]{2,1,0:T(8,128)(2,1)} %wi_hbm.1, bf16[1376,2048]{1,0:T(8,128)(2,1)} %wo_hbm.1), custom_call_target="tpu_custom_call" | custom-call | flops 8657043456 | bytes 17000000 | tf_op jit(solution)/shard_map/mlp/pallas_call | solution.py:462
  58.8 0.7 %copy.16 = bf16[64,2048]{1,0:T(8,128)(2,1)} copy(bf16[64,2048]{1,0:T(8,128)(2,1)S(1)} %mlp.1) | data formatting | bytes 524288
